TPU v7x, 128 devices: a whole 4x4x4 slice. The times are simulated.
128 devices in a mesh: rows: 16 (over z_lo, y, core), width: 8 (over z_hi, x).
Axes of the slice: x: 4, y: 4, z: 4 (z_hi: 2, z_lo: 2; z = z_hi * 2 + z_lo), core: 2. Of those that a mesh axis runs over, the one named last changes fastest.
Arguments:
- one_query: float32 [7168, 7168], P('rows', 'width'), may hold values from -0.09375 to 0.09375
- other_query: float32 [7168, 7168], P('rows', 'width'), may hold values from -0.0625 to 0.0625
- one_key: float32 [7168, 1024], P('rows', 'width'), may hold values from -0.09375 to 0.09375
- other_key: float32 [7168, 1024], P('rows', 'width'), may hold values from -0.0625 to 0.0625
- one_value: float32 [7168, 1024], P('rows', 'width'), may hold values from -0.09375 to 0.09375
- other_value: float32 [7168, 1024], P('rows', 'width'), may hold values from -0.0625 to 0.0625
- mix_share: float32 [7168], P('rows'), may hold values from 0.2 to 0.8
- norm_train: float32 [7168], P(('rows', 'width')), may hold values from 0.25 to 1.75
- norm_step: float32 [7168], P(('rows', 'width')), may hold values from -0.3 to 0.3
Outputs:
- final_query: bfloat16 [7168, 7168], P(None, 'width')
- final_key: bfloat16 [7168, 1024], P(None, 'width')
- final_value: bfloat16 [7168, 1024], P(None, 'width')
- column_query: float32 [7168], P('width')
- column_key: float32 [1024], P('width')
- column_value: float32 [1024], P('width')
- serve_norm: bfloat16 [7168], replicated
All inputs are finite; a program needn't handle non-finite values.
Results may differ from a plain program's by a relative error of at most 0.001.
Values may be sent and summed in bfloat16 or wider, within the bound.
A program may use at most 128 MiB of HBM per device.

v0:
```python
import jax
import jax.numpy as jnp
from jax import lax
from jax.experimental import pallas as pl
from jax.experimental.pallas import tpu as pltpu
from jax.sharding import PartitionSpec as P

MESH = pl.DeviceIdType.MESH
LANES = 128
WINDOW = 4
EARLY = 2


def kernel(
    n_rows,
    n_width,
    share_in,
    norm_train,
    norm_step,
    one_query,
    other_query,
    one_key,
    other_key,
    one_value,
    other_value,
    *refs,
):
    blocks = refs[: 2 + one_query.shape[1] // one_key.shape[1]]
    col_query, col_key, col_value, norm_all, first, second, share = refs[len(blocks) :][:7]
    part_early, part_late, in_sem, norm_send, norm_recv = refs[len(blocks) + 7 :][:5]
    slab_send, slab_recv, sum_send, sum_recv = refs[len(blocks) + 12 :][:4]
    ring_send, ring_recv, twin_send, twin_recv = refs[len(blocks) + 16 :]
    me = lax.axis_index("rows")
    lane = lax.axis_index("width")
    depth, wide = one_key.shape
    groups = [
        (one_key, other_key, blocks[0], col_key, 0),
        (one_value, other_value, blocks[1], col_value, 0),
    ] + [
        (one_query, other_query, blocks[2 + j], col_query, j * wide)
        for j in range(one_query.shape[1] // wide)
    ]
    tile = 64 if depth % 64 == 0 else 16
    half = depth // 2

    loads = []
    for g, (one, other, _, _, at) in enumerate(groups):
        a = pltpu.make_async_copy(one.at[:, pl.ds(at, wide)], first.at[g], in_sem.at[0, g])
        b = pltpu.make_async_copy(other.at[:, pl.ds(at, wide)], second.at[g], in_sem.at[1, g])
        loads.append((a, b))
        if g < WINDOW:
            a.start()
            b.start()

    norm_all[me, lane] = (norm_train[...] + norm_step[...]).reshape(1, -1)
    for at in range(0, depth, LANES):
        size = min(LANES, depth - at)
        line = share_in[pl.ds(at, size)].reshape(1, size)
        share[pl.ds(at, size), :] = jnp.broadcast_to(line, (LANES, size)).T

    barrier = pltpu.get_barrier_semaphore()
    for d in range(1, n_rows):
        pl.semaphore_signal(
            barrier, inc=1, device_id={"rows": lax.rem(me + d, n_rows)}, device_id_type=MESH
        )
    for d in range(1, n_width):
        pl.semaphore_signal(
            barrier, inc=1, device_id={"width": lax.rem(lane + d, n_width)}, device_id_type=MESH
        )
    pl.semaphore_wait(barrier, n_rows + n_width - 2)

    norm_copies = []
    for d in range(1, n_width):
        copy = pltpu.make_async_remote_copy(
            src_ref=norm_all.at[me, lane],
            dst_ref=norm_all.at[me, lane],
            send_sem=norm_send.at[d],
            recv_sem=norm_recv.at[d],
            device_id={"width": lax.rem(lane + d, n_width)},
            device_id_type=MESH,
        )
        copy.start()
        norm_copies.append(copy)

    def send_sums(part, kind):
        copies = []
        for d in range(1, n_rows):
            copy = pltpu.make_async_remote_copy(
                src_ref=part.at[me],
                dst_ref=part.at[me],
                send_sem=sum_send.at[kind, d],
                recv_sem=sum_recv.at[kind, d],
                device_id={"rows": lax.rem(me + d, n_rows)},
                device_id_type=MESH,
            )
            copy.start()
            copies.append(copy)
        return copies

    for g in range(len(groups)):
        for load in loads[g]:
            load.wait()
        for load in loads[g + WINDOW] if g + WINDOW < len(groups) else ():
            load.start()

        def mix(i, acc):
            rows = pl.ds(pl.multiple_of(i * tile, tile), tile)
            s = share[rows, :]
            s = jnp.concatenate([s] * (wide // LANES), axis=1)
            r = s * first[g, rows, :] + (1.0 - s) * second[g, rows, :]
            first[g, rows, :] = r
            return acc + jnp.sum((r * r).reshape(tile // 8, 8, wide), axis=0)

        acc = lax.fori_loop(0, depth // tile, mix, jnp.zeros((8, wide), jnp.float32))
        line = jnp.sum(acc, axis=0, keepdims=True)
        if g < EARLY:
            part_early[me, g] = line
        else:
            part_late[me, g - EARLY] = line
        if g == EARLY:
            early_copies = send_sums(part_early, 0)

    late_copies = send_sums(part_late, 1)

    for copy in norm_copies:
        copy.wait_recv()
    slab_copies = []
    for d in range(1, n_rows):
        copy = pltpu.make_async_remote_copy(
            src_ref=norm_all.at[me],
            dst_ref=norm_all.at[me],
            send_sem=slab_send.at[d],
            recv_sem=slab_recv.at[d],
            device_id={"rows": lax.rem(me + d, n_rows)},
            device_id_type=MESH,
        )
        copy.start()
        slab_copies.append(copy)

    core = lax.rem(me, 2)
    chip = me // 2
    chips = n_rows // 2
    reach = chips // 2

    def fold(c):
        return jnp.where(c < reach, c, 3 * reach - 1 - c)

    place = fold(chip)

    def device_at(step):
        return fold(lax.rem(place + step + chips, chips)) * 2 + core

    twin = me + 1 - 2 * core
    ahead = (device_at(1), device_at(-1))
    waits = []

    def region(g, owner, way, hop):
        if hop < reach:
            rows = pl.ds(pl.multiple_of(owner * depth, half), depth)
        else:
            rows = pl.ds(pl.multiple_of(owner * depth + way * half, half), half)
        return blocks[g].at[rows, :]

    def ring_copy(g, owner, way, hop):
        ref = region(g, owner, way, hop)
        copy = pltpu.make_async_remote_copy(
            src_ref=ref,
            dst_ref=ref,
            send_sem=ring_send.at[way, hop - 1, g],
            recv_sem=ring_recv.at[way, hop - 1, g],
            device_id={"rows": ahead[way]},
            device_id_type=MESH,
        )
        copy.start()
        return copy

    def twin_copy(g, owner, way, hop, slot):
        ref = region(g, owner, way, hop)
        copy = pltpu.make_async_remote_copy(
            src_ref=ref,
            dst_ref=ref,
            send_sem=twin_send.at[slot, g],
            recv_sem=twin_recv.at[slot, g],
            device_id={"rows": twin},
            device_id_type=MESH,
        )
        copy.start()
        waits.append(copy)

    flying = {}
    for g, (_, _, out, col, at) in enumerate(groups):
        if g in (0, EARLY):
            for copy in early_copies if g == 0 else late_copies:
                copy.wait_recv()
        part, line = (part_early, g) if g < EARLY else (part_late, g - EARLY)
        total = part[0, line]
        for p in range(1, n_rows):
            total = total + part[p, line]
        scale = jnp.sqrt(total)
        col[pl.ds(at, wide)] = scale.reshape(wide)
        inverse = 1.0 / scale

        def narrow(i, carry):
            rows = pl.ds(pl.multiple_of(i * tile, tile), tile)
            here = pl.ds(pl.multiple_of(me * depth + i * tile, tile), tile)
            out[here, :] = (first[g, rows, :] * inverse).astype(out.dtype)
            return carry

        lax.fori_loop(0, depth // tile, narrow, 0)
        for way in range(2):
            flying[way, 1, g] = ring_copy(g, me, way, 1)
        twin_copy(g, me, 0, 0, 0)

    for hop in range(1, reach + 1):
        for g in range(len(groups)):
            for way in range(2):
                copy = flying[way, hop, g]
                copy.wait_recv()
                owner = device_at(-hop if way == 0 else hop)
                if hop < reach:
                    flying[way, hop + 1, g] = ring_copy(g, owner, way, hop + 1)
                twin_copy(g, owner, way, hop, 1 + 2 * (hop - 1) + way)

    for copy in flying.values():
        copy.wait_send()
    for copy in waits:
        copy.wait()
    for copy in norm_copies + early_copies + late_copies:
        copy.wait_send()
    for copy in slab_copies:
        copy.wait()


def store(*refs):
    outs, sem = refs[-8:-1], refs[-1]
    blocks, small = refs[:-12], refs[-12:-8]
    wide = blocks[0].shape[1]
    pairs = [(blocks[0], outs[1]), (blocks[1], outs[2])] + list(zip(small, outs[3:]))
    for j, block in enumerate(blocks[2:]):
        pairs.append((block, outs[0].at[:, pl.ds(j * wide, wide)]))
    copies = [pltpu.make_async_copy(src, dst, sem.at[i]) for i, (src, dst) in enumerate(pairs)]
    for copy in copies:
        copy.start()
    for copy in copies:
        copy.wait()


def solution(mesh):
    n_rows, n_width = mesh.shape["rows"], mesh.shape["width"]

    def shards(
        one_query,
        other_query,
        one_key,
        other_key,
        one_value,
        other_value,
        mix_share,
        norm_train,
        norm_step,
    ):
        depth, wide = one_key.shape
        wide_query = one_query.shape[1]
        count = 2 + wide_query // wide
        piece = norm_train.shape[0]
        total = depth * n_rows
        reach = n_rows // 4
        hbm = pl.BlockSpec(memory_space=pltpu.HBM)
        vmem = pl.BlockSpec(memory_space=pltpu.VMEM)
        dma = pltpu.SemaphoreType.DMA
        out_shape = (pltpu.VMEM((total, wide), jnp.bfloat16),) * count + (
            pltpu.VMEM((wide_query,), jnp.float32),
            pltpu.VMEM((wide,), jnp.float32),
            pltpu.VMEM((wide,), jnp.float32),
            pltpu.VMEM((n_rows, n_width, 1, piece), jnp.float32),
        )
        gathered = pl.pallas_call(
            lambda *refs: kernel(n_rows, n_width, *refs),
            out_shape=out_shape,
            in_specs=[vmem] * 3 + [hbm] * 6,
            out_specs=[vmem] * (count + 4),
            scratch_shapes=[
                pltpu.VMEM((count, depth, wide), jnp.float32),
                pltpu.VMEM((count, depth, wide), jnp.float32),
                pltpu.VMEM((depth, LANES), jnp.float32),
                pltpu.VMEM((n_rows, EARLY, 1, wide), jnp.float32),
                pltpu.VMEM((n_rows, count - EARLY, 1, wide), jnp.float32),
                dma((2, count)),
                dma((n_width,)),
                dma((n_width,)),
                dma((n_rows,)),
                dma((n_rows,)),
                dma((2, n_rows)),
                dma((2, n_rows)),
                dma((2, reach, count)),
                dma((2, reach, count)),
                dma((1 + 2 * reach, count)),
                dma((1 + 2 * reach, count)),
            ],
            compiler_params=pltpu.CompilerParams(
                collective_id=0, has_side_effects=True, vmem_limit_bytes=24 * 1024 * 1024
            ),
        )(mix_share, norm_train, norm_step, one_query, other_query, one_key, other_key, one_value, other_value)
        final_query, final_key, final_value, col_query, col_key, col_value, norm_all = pl.pallas_call(
            store,
            out_shape=(
                jax.ShapeDtypeStruct((total, wide_query), jnp.bfloat16),
                jax.ShapeDtypeStruct((total, wide), jnp.bfloat16),
                jax.ShapeDtypeStruct((total, wide), jnp.bfloat16),
            )
            + tuple(jax.ShapeDtypeStruct(o.shape, o.dtype) for o in out_shape[count:]),
            in_specs=[vmem] * (count + 4),
            out_specs=[hbm] * 7,
            scratch_shapes=[dma((count + 4,))],
            compiler_params=pltpu.CompilerParams(vmem_limit_bytes=1024 * 1024),
        )(*gathered)
        serve_norm = norm_all[..., 0, :].astype(jnp.bfloat16).reshape(-1)
        return (
            final_query,
            final_key,
            final_value,
            col_query,
            col_key,
            col_value,
            serve_norm,
        )

    wide_spec = P("rows", "width")
    in_specs = (wide_spec,) * 6 + (P("rows"), P(("rows", "width")), P(("rows", "width")))
    out_specs = (P(None, "width"),) * 3 + (P("width"),) * 3 + (P(),)
    return jax.shard_map(shards, mesh=mesh, in_specs=in_specs, out_specs=out_specs, check_vma=False)
```

profile of v0, /device:TPU:1, one launch (start us, length us, event | category | flops | bytes accessed | tf_op | source)
XLA Modules:
  0.0 115.6 jit_solution(11959430460652330346)
XLA Ops:
  0.6 0.0 copy-start
  0.6 1.4 %copy-done = f32[448,896]{1,0:T(8,128)S(1)} copy-done((f32[448,896]{1,0:T(8,128)S(1)}, f32[448,896]{1,0:T(8,128)}, u32[]{:S(2)}) %copy-start) | copy-done | bytes 1605656
  2.1 0.0 copy-start.1
  2.1 1.4 %copy-done.1 = f32[448,896]{1,0:T(8,128)S(1)} copy-done((f32[448,896]{1,0:T(8,128)S(1)}, f32[448,896]{1,0:T(8,128)}, u32[]{:S(2)}) %copy-start.1) | copy-done | bytes 1605656
  3.5 0.0 copy-start.2
  3.5 0.9 copy-done.2
  4.4 0.0 copy-start.3
  4.4 0.9 copy-done.3
  5.4 0.0 copy-start.4
  5.4 0.9 copy-done.4
  6.3 0.0 copy-start.5
  6.3 0.9 copy-done.5
  7.2 0.0 copy-start.6
  7.2 0.7 copy-done.6
  7.9 0.0 copy-start.7
  7.9 0.7 copy-done.7
  8.6 0.0 copy-start.8
  8.6 0.7 copy-done.8
  9.2 99.5 %shard_map.144 = (bf16[7168,128]{1,0:T(8,128)(2,1)S(1)}, bf16[7168,128]{1,0:T(8,128)(2,1)S(1)}, bf16[7168,128]{1,0:T(8,128)(2,1)S(1)}, bf16[7168,128]{1,0:T(8,12...) custom-call(f32[448]{0:T(512)S(1)} %copy-done.6, ...), custom_call_target="tpu_custom_call" | custom-call | tf_op jit(solution)/shard_map/pallas_call | solution.py:277
  108.7 5.9 %shard_map.145 = (bf16[7168,896]{1,0:T(8,128)(2,1)}, bf16[7168,128]{1,0:T(8,128)(2,1)}, bf16[7168,128]{1,0:T(8,128)(2,1)}, f32[896]{0:T(1024)}, f32[128]{0:T(128...) custom-call(bf16[7168,128]{1,0:T(8,128)(2,1)S(1)} %get-tuple-element.27.refs_0_, ...), custom_call_target="tpu_custom_call" | custom-call | tf_op jit(solution)/shard_map/pallas_call | solution.py:304
  114.7 0.2 convert_reduce_fusion
  114.9 0.7 convert_element_type.8
Async XLA Ops:
  0.6 1.4 %copy-start = (f32[448,896]{1,0:T(8,128)S(1)}, f32[448,896]{1,0:T(8,128)}, u32[]{:S(2)}) copy-start(f32[448,896]{1,0:T(8,128)} %refs_3_.1) | copy-start | bytes 4816900
  2.1 1.4 %copy-start.1 = (f32[448,896]{1,0:T(8,128)S(1)}, f32[448,896]{1,0:T(8,128)}, u32[]{:S(2)}) copy-start(f32[448,896]{1,0:T(8,128)} %refs_4_.1) | copy-start | bytes 4816900
  3.5 0.9 copy-start.2
  4.4 0.9 copy-start.3
  5.4 0.9 copy-start.4
  6.3 0.9 copy-start.5
  7.2 0.7 copy-start.6
  7.9 0.7 copy-start.7
  8.6 0.7 copy-start.8
where the time goes:
time: 116 us
  Pallas kernels  105 us (91%)
  local copies, waits for them, and re-layouts  9.29 us (8%)
    pallas_call x1, Pallas kernels, shards(): pl.pallas_call(lambda *refs: kernel(n_rows, n_width, *refs), out_shape=ou...  99.5 us
    unnamed x18, local copies, waits for them, and re-layouts  8.57 us
    pallas_call x1, Pallas kernels, shards(): pl.pallas_call(store, out_shape=(jax.ShapeDtypeStruct((total, wide_query)...  5.93 us

commit v1 on v0

v1 whole, which is shorter than its diff:
```python
import jax
import jax.numpy as jnp
from jax import lax
from jax.experimental import pallas as pl
from jax.experimental.pallas import tpu as pltpu
from jax.sharding import PartitionSpec as P

MESH = pl.DeviceIdType.MESH
LANES = 128
CIRCLE = 4
UP, DOWN, ACROSS = 0, 1, 2


def split_groups(count):
    first = [g for g in range(count) if g % 2 == 0]
    return first, [g for g in range(count) if g % 2]


def plan(count, cross_first):
    free = [0.0, 0.0, 0.0]
    flying = []

    def send(now, item):
        link, _, hop, _ = item
        half = hop == 2 if link != ACROSS else hop >= 3
        free[link] = max(free[link], now) + (0.5 if half else 1.0)
        flying.append((free[link], len(flying), item))

    for g in range(count):
        send(0.0, (UP, 0, 1, g))
        send(0.0, (DOWN, 0, 1, g))
        send(0.0, (ACROSS, 0, 0, g))
    order = []
    while flying:
        flying.sort()
        now, _, item = flying.pop(0)
        now += 0.5
        steps = followers(item, cross_first)
        order.append((item, steps))
        for step in steps:
            send(now, step)
    return order


def followers(item, cross_first):
    link, far, hop, g = item
    if link == ACROSS:
        return [(UP, 1, 1, g), (DOWN, 1, 1, g)] if g in cross_first else []
    steps = [(link, far, 2, g)] if hop == 1 else []
    if g not in cross_first:
        steps.append((ACROSS, 0, 1 + link if hop == 1 else 3 + link, g))
    return steps


def kernel(
    n_rows,
    n_width,
    share_in,
    norm_train,
    norm_step,
    one_query,
    other_query,
    one_key,
    other_key,
    one_value,
    other_value,
    *refs,
):
    blocks = refs[: 2 + one_query.shape[1] // one_key.shape[1]]
    col_query, col_key, col_value, norm_all, first, second, share = refs[len(blocks) :][:7]
    line, train, step, part, in_sem, small_sem = refs[len(blocks) + 7 :][:6]
    norm_send, norm_recv, slab_send, slab_recv, sum_send, sum_recv = refs[len(blocks) + 13 :][:6]
    ring_send, ring_recv, pair_send, pair_recv, twin_send, twin_recv = refs[len(blocks) + 19 :]
    me = lax.axis_index("rows")
    lane = lax.axis_index("width")
    depth, wide = one_key.shape
    groups = [
        (one_key, other_key, blocks[0], col_key, 0),
        (one_value, other_value, blocks[1], col_value, 0),
    ] + [
        (one_query, other_query, blocks[2 + j], col_query, j * wide)
        for j in range(one_query.shape[1] // wide)
    ]
    count = len(groups)
    tile = 64 if depth % 64 == 0 else 16
    half = depth // 2

    small = []
    for i, (src, dst) in enumerate(((share_in, line), (norm_train, train), (norm_step, step))):
        small.append(pltpu.make_async_copy(src, dst, small_sem.at[i]))
        small[-1].start()
    loads = []
    for g, (one, other, _, _, at) in enumerate(groups):
        a = pltpu.make_async_copy(one.at[:, pl.ds(at, wide)], first.at[g], in_sem.at[0, g])
        b = pltpu.make_async_copy(other.at[:, pl.ds(at, wide)], second.at[g], in_sem.at[1, g])
        loads.append((a, b))
        a.start()
        b.start()

    barrier = pltpu.get_barrier_semaphore()
    for d in range(1, n_rows):
        pl.semaphore_signal(
            barrier, inc=1, device_id={"rows": lax.rem(me + d, n_rows)}, device_id_type=MESH
        )
    for d in range(1, n_width):
        pl.semaphore_signal(
            barrier, inc=1, device_id={"width": lax.rem(lane + d, n_width)}, device_id_type=MESH
        )

    for copy in small:
        copy.wait()
    norm_all[me, lane] = (train[...] + step[...]).reshape(1, -1)
    for at in range(0, depth, LANES):
        size = min(LANES, depth - at)
        piece = line[pl.ds(at, size)].reshape(1, size)
        share[pl.ds(at, size), :] = jnp.broadcast_to(piece, (LANES, size)).T

    for g in range(count):
        for load in loads[g]:
            load.wait()

        def mix(i, acc):
            rows = pl.ds(pl.multiple_of(i * tile, tile), tile)
            s = share[rows, :]
            s = jnp.concatenate([s] * (wide // LANES), axis=1)
            r = s * first[g, rows, :] + (1.0 - s) * second[g, rows, :]
            first[g, rows, :] = r
            return acc + jnp.sum((r * r).reshape(tile // 8, 8, wide), axis=0)

        acc = lax.fori_loop(0, depth // tile, mix, jnp.zeros((8, wide), jnp.float32))
        part[me, pl.ds(g, 1), :] = jnp.sum(acc, axis=0, keepdims=True)

    pl.semaphore_wait(barrier, n_rows + n_width - 2)

    sums = []
    for d in range(1, n_rows):
        copy = pltpu.make_async_remote_copy(
            src_ref=part.at[me],
            dst_ref=part.at[me],
            send_sem=sum_send.at[d],
            recv_sem=sum_recv.at[d],
            device_id={"rows": lax.rem(me + d, n_rows)},
            device_id_type=MESH,
        )
        copy.start()
        sums.append(copy)
    norm_copies = []
    for d in range(1, n_width):
        copy = pltpu.make_async_remote_copy(
            src_ref=norm_all.at[me, lane],
            dst_ref=norm_all.at[me, lane],
            send_sem=norm_send.at[d],
            recv_sem=norm_recv.at[d],
            device_id={"width": lax.rem(lane + d, n_width)},
            device_id_type=MESH,
        )
        copy.start()
        norm_copies.append(copy)

    core = me % 2
    place = (me // 2) % CIRCLE
    side = me // (2 * CIRCLE)

    def device(sides, steps):
        return ((side + sides) % 2 * CIRCLE + (place + steps + CIRCLE) % CIRCLE) * 2 + core

    twin = me + 1 - 2 * core
    target = {UP: device(0, 1), DOWN: device(0, -1), ACROSS: device(1, 0)}
    waits = []

    def whole(owner):
        return pl.ds(pl.multiple_of(owner * depth, half), depth)

    def part_of(owner, way):
        return pl.ds(pl.multiple_of(owner * depth + way * half, half), half)

    def rows_of(item, sender):
        link, far, hop, _ = item
        if link == ACROSS:
            side_of = 0 if sender else 1
            if hop >= 3:
                return part_of(device(side_of, 2), hop - 3)
            return whole(device(side_of, (0, -1, 1)[hop]))
        away = hop - 1 if sender else hop
        owner = device(far, -away if link == UP else away)
        return whole(owner) if hop == 1 else part_of(owner, link)

    def remote(item, sender):
        link, far, hop, g = item
        ref = blocks[g].at[rows_of(item, sender), :]
        if link == ACROSS:
            sems = pair_send.at[hop, g], pair_recv.at[hop, g]
        else:
            sems = ring_send.at[link, far, hop - 1, g], ring_recv.at[link, far, hop - 1, g]
        return pltpu.make_async_remote_copy(
            src_ref=ref,
            dst_ref=ref,
            send_sem=sems[0],
            recv_sem=sems[1],
            device_id={"rows": target[link]},
            device_id_type=MESH,
        )

    def send(item):
        copy = remote(item, True)
        copy.start()
        waits.append(copy)

    twins = []

    def share_with_twin(g, rows, slot):
        ref = blocks[g].at[rows, :]
        copy = pltpu.make_async_remote_copy(
            src_ref=ref,
            dst_ref=ref,
            send_sem=twin_send.at[slot, g],
            recv_sem=twin_recv.at[slot, g],
            device_id={"rows": twin},
            device_id_type=MESH,
        )
        copy.start()
        twins.append(copy)

    for copy in sums:
        copy.wait_recv()
    total = part[0]
    for p in range(1, n_rows):
        total = total + part[p]
    scale = jnp.sqrt(total)
    inverse = 1.0 / scale

    def release(g):
        send((ACROSS, 0, 0, g))
        send((UP, 0, 1, g))
        send((DOWN, 0, 1, g))
        share_with_twin(g, whole(me), 0)

    for g, (_, _, out, col, at) in enumerate(groups):
        col[pl.ds(at, wide)] = scale[g : g + 1, :].reshape(wide)
        by = inverse[g : g + 1, :]

        def narrow(i, carry):
            rows = pl.ds(pl.multiple_of(i * tile, tile), tile)
            here = pl.ds(pl.multiple_of(me * depth + i * tile, tile), tile)
            out[here, :] = (first[g, rows, :] * by).astype(out.dtype)
            return carry

        lax.fori_loop(0, depth // tile, narrow, 0)
        if g:
            release(g - 1)
    release(count - 1)

    for copy in norm_copies:
        copy.wait_recv()
    slab_copies = []
    for d in range(1, n_rows):
        copy = pltpu.make_async_remote_copy(
            src_ref=norm_all.at[me],
            dst_ref=norm_all.at[me],
            send_sem=slab_send.at[d],
            recv_sem=slab_recv.at[d],
            device_id={"rows": lax.rem(me + d, n_rows)},
            device_id_type=MESH,
        )
        copy.start()
        slab_copies.append(copy)

    cross_first, _ = split_groups(count)
    slots = [1] * count
    for item, steps in plan(count, cross_first):
        g = item[3]
        remote(item, False).wait_recv()
        for step_on in steps:
            send(step_on)
        share_with_twin(g, rows_of(item, False), slots[g])
        slots[g] += 1

    for copy in waits:
        copy.wait_send()
    for copy in twins:
        copy.wait()
    for copy in norm_copies + sums:
        copy.wait_send()
    for copy in slab_copies:
        copy.wait()


def store(*refs):
    outs, sem = refs[-8:-1], refs[-1]
    blocks, small = refs[:-12], refs[-12:-8]
    wide = blocks[0].shape[1]
    pairs = [(blocks[0], outs[1]), (blocks[1], outs[2])] + list(zip(small, outs[3:]))
    for j, block in enumerate(blocks[2:]):
        pairs.append((block, outs[0].at[:, pl.ds(j * wide, wide)]))
    copies = [pltpu.make_async_copy(src, dst, sem.at[i]) for i, (src, dst) in enumerate(pairs)]
    for copy in copies:
        copy.start()
    for copy in copies:
        copy.wait()


def solution(mesh):
    n_rows, n_width = mesh.shape["rows"], mesh.shape["width"]

    def shards(
        one_query,
        other_query,
        one_key,
        other_key,
        one_value,
        other_value,
        mix_share,
        norm_train,
        norm_step,
    ):
        depth, wide = one_key.shape
        wide_query = one_query.shape[1]
        count = 2 + wide_query // wide
        piece = norm_train.shape[0]
        total = depth * n_rows
        hbm = pl.BlockSpec(memory_space=pltpu.HBM)
        vmem = pl.BlockSpec(memory_space=pltpu.VMEM)
        dma = pltpu.SemaphoreType.DMA
        out_shape = (pltpu.VMEM((total, wide), jnp.bfloat16),) * count + (
            pltpu.VMEM((wide_query,), jnp.float32),
            pltpu.VMEM((wide,), jnp.float32),
            pltpu.VMEM((wide,), jnp.float32),
            pltpu.VMEM((n_rows, n_width, 1, piece), jnp.float32),
        )
        gathered = pl.pallas_call(
            lambda *refs: kernel(n_rows, n_width, *refs),
            out_shape=out_shape,
            in_specs=[hbm] * 9,
            out_specs=[vmem] * (count + 4),
            scratch_shapes=[
                pltpu.VMEM((count, depth, wide), jnp.float32),
                pltpu.VMEM((count, depth, wide), jnp.float32),
                pltpu.VMEM((depth, LANES), jnp.float32),
                pltpu.VMEM((depth,), jnp.float32),
                pltpu.VMEM((piece,), jnp.float32),
                pltpu.VMEM((piece,), jnp.float32),
                pltpu.VMEM((n_rows, count, wide), jnp.float32),
                dma((2, count)),
                dma((3,)),
                dma((n_width,)),
                dma((n_width,)),
                dma((n_rows,)),
                dma((n_rows,)),
                dma((n_rows,)),
                dma((n_rows,)),
                dma((2, 2, 2, count)),
                dma((2, 2, 2, count)),
                dma((5, count)),
                dma((5, count)),
                dma((10, count)),
                dma((10, count)),
            ],
            compiler_params=pltpu.CompilerParams(
                collective_id=0, has_side_effects=True, vmem_limit_bytes=44 * 1024 * 1024
            ),
        )(mix_share, norm_train, norm_step, one_query, other_query, one_key, other_key, one_value, other_value)
        final_query, final_key, final_value, col_query, col_key, col_value, norm_all = pl.pallas_call(
            store,
            out_shape=(
                jax.ShapeDtypeStruct((total, wide_query), jnp.bfloat16),
                jax.ShapeDtypeStruct((total, wide), jnp.bfloat16),
                jax.ShapeDtypeStruct((total, wide), jnp.bfloat16),
            )
            + tuple(jax.ShapeDtypeStruct(o.shape, o.dtype) for o in out_shape[count:]),
            in_specs=[vmem] * (count + 4),
            out_specs=[hbm] * 7,
            scratch_shapes=[dma((count + 4,))],
            compiler_params=pltpu.CompilerParams(vmem_limit_bytes=1024 * 1024),
        )(*gathered)
        serve_norm = norm_all[..., 0, :].astype(jnp.bfloat16).reshape(-1)
        return (
            final_query,
            final_key,
            final_value,
            col_query,
            col_key,
            col_value,
            serve_norm,
        )

    wide_spec = P("rows", "width")
    in_specs = (wide_spec,) * 6 + (P("rows"), P(("rows", "width")), P(("rows", "width")))
    out_specs = (P(None, "width"),) * 3 + (P("width"),) * 3 + (P(),)
    return jax.shard_map(shards, mesh=mesh, in_specs=in_specs, out_specs=out_specs, check_vma=False)
```

time: 116 us -> 81.3 us (0.70)
  Pallas kernels: 105 us -> 79.6 us
  local copies, waits for them, and re-layouts: 9.29 us -> 0.72 us
    pallas_call x1, Pallas kernels: 99.5 us -> 73.7 us  [shards(): pl.pallas_call(lambda *refs: kernel(n_rows, n_width, *refs), out_shape=ou...]
    unnamed x18 -> x0, local copies, waits for them, and re-layouts: 8.57 us -> none
where the time goes in v1:
time: 81.3 us; the launch traced here: 81.1 us
  Pallas kernels  79.6 us (98%)
    pallas_call x1, Pallas kernels, shards(): pl.pallas_call(lambda *refs: kernel(n_rows, n_width, *refs), out_shape=ou...  73.7 us
    pallas_call x1, Pallas kernels, shards(): pl.pallas_call(store, out_shape=(jax.ShapeDtypeStruct((total, wide_query)...  5.93 us

profile of v1, /device:TPU:1, one launch (start us, length us, event | category | flops | bytes accessed | tf_op | source)
XLA Modules:
  0.0 81.1 jit_solution(3570490903152393925)
XLA Ops:
  0.6 73.7 %shard_map.144 = (bf16[7168,128]{1,0:T(8,128)(2,1)S(1)}, bf16[7168,128]{1,0:T(8,128)(2,1)S(1)}, bf16[7168,128]{1,0:T(8,128)(2,1)S(1)}, bf16[7168,128]{1,0:T(8,12...) custom-call(f32[448]{0:T(512)} %refs_0_.1, ...), custom_call_target="tpu_custom_call" | custom-call | tf_op jit(solution)/shard_map/pallas_call | solution.py:330
  74.3 5.9 %shard_map.145 = (bf16[7168,896]{1,0:T(8,128)(2,1)}, bf16[7168,128]{1,0:T(8,128)(2,1)}, bf16[7168,128]{1,0:T(8,128)(2,1)}, f32[896]{0:T(1024)}, f32[128]{0:T(128...) custom-call(bf16[7168,128]{1,0:T(8,128)(2,1)S(1)} %get-tuple-element.27.refs_0_, ...), custom_call_target="tpu_custom_call" | custom-call | tf_op jit(solution)/shard_map/pallas_call | solution.py:362
  80.2 0.2 convert_reduce_fusion
  80.4 0.7 convert_element_type.8

commit v2 on v1

--- a/solution.py
+++ b/solution.py
@@ -21,9 +21,8 @@
     flying = []
 
     def send(now, item):
-        link, _, hop, _ = item
-        half = hop == 2 if link != ACROSS else hop >= 3
-        free[link] = max(free[link], now) + (0.5 if half else 1.0)
+        link = item[0]
+        free[link] = max(free[link], now) + (1.0 if is_whole(item) else 0.5)
         flying.append((free[link], len(flying), item))
 
     for g in range(count):
@@ -40,6 +39,11 @@
         for step in steps:
             send(now, step)
     return order
+
+
+def is_whole(item):
+    link, _, hop, _ = item
+    return hop < 3 if link == ACROSS else hop == 1
 
 
 def followers(item, cross_first):
@@ -67,10 +71,10 @@
     *refs,
 ):
     blocks = refs[: 2 + one_query.shape[1] // one_key.shape[1]]
-    col_query, col_key, col_value, norm_all, first, second, share = refs[len(blocks) :][:7]
-    line, train, step, part, in_sem, small_sem = refs[len(blocks) + 7 :][:6]
-    norm_send, norm_recv, slab_send, slab_recv, sum_send, sum_recv = refs[len(blocks) + 13 :][:6]
-    ring_send, ring_recv, pair_send, pair_recv, twin_send, twin_recv = refs[len(blocks) + 19 :]
+    col_query, col_key, col_value, norm_all, mixed, share = refs[len(blocks) :][:6]
+    line, train, step, part, in_sem, small_sem = refs[len(blocks) + 6 :][:6]
+    norm_sem, slab_sem, sum_sem, send_sem = refs[len(blocks) + 12 :][:4]
+    ring_recv, pair_recv, twin_sem = refs[len(blocks) + 16 :]
     me = lax.axis_index("rows")
     lane = lax.axis_index("width")
     depth, wide = one_key.shape
@@ -85,15 +89,16 @@
     tile = 64 if depth % 64 == 0 else 16
     half = depth // 2
 
+    def drain(ref, sem):
+        pltpu.make_async_copy(ref, ref, sem).wait()
+
     small = []
     for i, (src, dst) in enumerate(((share_in, line), (norm_train, train), (norm_step, step))):
         small.append(pltpu.make_async_copy(src, dst, small_sem.at[i]))
         small[-1].start()
-    loads = []
     for g, (one, other, _, _, at) in enumerate(groups):
-        a = pltpu.make_async_copy(one.at[:, pl.ds(at, wide)], first.at[g], in_sem.at[0, g])
-        b = pltpu.make_async_copy(other.at[:, pl.ds(at, wide)], second.at[g], in_sem.at[1, g])
-        loads.append((a, b))
+        a = pltpu.make_async_copy(one.at[:, pl.ds(at, wide)], mixed.at[g, 0], in_sem.at[g])
+        b = pltpu.make_async_copy(other.at[:, pl.ds(at, wide)], mixed.at[g, 1], in_sem.at[g])
         a.start()
         b.start()
 
@@ -116,15 +121,14 @@
         share[pl.ds(at, size), :] = jnp.broadcast_to(piece, (LANES, size)).T
 
     for g in range(count):
-        for load in loads[g]:
-            load.wait()
+        drain(mixed.at[g], in_sem.at[g])
 
         def mix(i, acc):
             rows = pl.ds(pl.multiple_of(i * tile, tile), tile)
             s = share[rows, :]
             s = jnp.concatenate([s] * (wide // LANES), axis=1)
-            r = s * first[g, rows, :] + (1.0 - s) * second[g, rows, :]
-            first[g, rows, :] = r
+            r = s * mixed[g, 0, rows, :] + (1.0 - s) * mixed[g, 1, rows, :]
+            mixed[g, 0, rows, :] = r
             return acc + jnp.sum((r * r).reshape(tile // 8, 8, wide), axis=0)
 
         acc = lax.fori_loop(0, depth // tile, mix, jnp.zeros((8, wide), jnp.float32))
@@ -132,30 +136,24 @@
 
     pl.semaphore_wait(barrier, n_rows + n_width - 2)
 
-    sums = []
-    for d in range(1, n_rows):
-        copy = pltpu.make_async_remote_copy(
-            src_ref=part.at[me],
-            dst_ref=part.at[me],
-            send_sem=sum_send.at[d],
-            recv_sem=sum_recv.at[d],
-            device_id={"rows": lax.rem(me + d, n_rows)},
-            device_id_type=MESH,
-        )
-        copy.start()
-        sums.append(copy)
-    norm_copies = []
-    for d in range(1, n_width):
-        copy = pltpu.make_async_remote_copy(
-            src_ref=norm_all.at[me, lane],
-            dst_ref=norm_all.at[me, lane],
-            send_sem=norm_send.at[d],
-            recv_sem=norm_recv.at[d],
-            device_id={"width": lax.rem(lane + d, n_width)},
-            device_id_type=MESH,
-        )
-        copy.start()
-        norm_copies.append(copy)
+    def to_others(ref, sems, axis, mine, size):
+        for d in range(1, size):
+            pltpu.make_async_remote_copy(
+                src_ref=ref,
+                dst_ref=ref,
+                send_sem=sems.at[0],
+                recv_sem=sems.at[1],
+                device_id={axis: lax.rem(mine + d, size)},
+                device_id_type=MESH,
+            ).start()
+
+    to_others(part.at[me], sum_sem, "rows", me, n_rows)
+    to_others(norm_all.at[me, lane], norm_sem, "width", lane, n_width)
+
+    cross_first, _ = split_groups(count)
+
+    def bucket(g):
+        return 2 * g // (count + 1)
 
     core = me % 2
     place = (me // 2) % CIRCLE
@@ -166,8 +164,6 @@
 
     twin = me + 1 - 2 * core
     target = {UP: device(0, 1), DOWN: device(0, -1), ACROSS: device(1, 0)}
-    waits = []
-
     def whole(owner):
         return pl.ds(pl.multiple_of(owner * depth, half), depth)
 
@@ -189,40 +185,39 @@
         link, far, hop, g = item
         ref = blocks[g].at[rows_of(item, sender), :]
         if link == ACROSS:
-            sems = pair_send.at[hop, g], pair_recv.at[hop, g]
+            arrived = pair_recv.at[hop, g]
         else:
-            sems = ring_send.at[link, far, hop - 1, g], ring_recv.at[link, far, hop - 1, g]
+            arrived = ring_recv.at[link, far, hop - 1, g]
         return pltpu.make_async_remote_copy(
             src_ref=ref,
             dst_ref=ref,
-            send_sem=sems[0],
-            recv_sem=sems[1],
+            send_sem=send_sem.at[link, bucket(g)],
+            recv_sem=arrived,
             device_id={"rows": target[link]},
             device_id_type=MESH,
         )
 
+    sent = {}
+
     def send(item):
-        copy = remote(item, True)
-        copy.start()
-        waits.append(copy)
-
-    twins = []
-
-    def share_with_twin(g, rows, slot):
+        remote(item, True).start()
+        link, _, hop, g = item
+        key = link, bucket(g)
+        sent[key] = sent.get(key, 0) + (depth if is_whole(item) else half)
+
+    def share_with_twin(g, rows):
         ref = blocks[g].at[rows, :]
-        copy = pltpu.make_async_remote_copy(
+        pltpu.make_async_remote_copy(
             src_ref=ref,
             dst_ref=ref,
-            send_sem=twin_send.at[slot, g],
-            recv_sem=twin_recv.at[slot, g],
+            send_sem=twin_sem.at[0, g],
+            recv_sem=twin_sem.at[1, g],
             device_id={"rows": twin},
             device_id_type=MESH,
-        )
-        copy.start()
-        twins.append(copy)
-
-    for copy in sums:
-        copy.wait_recv()
+        ).start()
+
+    others = part.at[pl.ds(0, n_rows - 1)]
+    drain(others, sum_sem.at[1])
     total = part[0]
     for p in range(1, n_rows):
         total = total + part[p]
@@ -233,7 +228,7 @@
         send((ACROSS, 0, 0, g))
         send((UP, 0, 1, g))
         send((DOWN, 0, 1, g))
-        share_with_twin(g, whole(me), 0)
+        share_with_twin(g, whole(me))
 
     for g, (_, _, out, col, at) in enumerate(groups):
         col[pl.ds(at, wide)] = scale[g : g + 1, :].reshape(wide)
@@ -242,7 +237,7 @@
         def narrow(i, carry):
             rows = pl.ds(pl.multiple_of(i * tile, tile), tile)
             here = pl.ds(pl.multiple_of(me * depth + i * tile, tile), tile)
-            out[here, :] = (first[g, rows, :] * by).astype(out.dtype)
+            out[here, :] = (mixed[g, 0, rows, :] * by).astype(out.dtype)
             return carry
 
         lax.fori_loop(0, depth // tile, narrow, 0)
@@ -250,39 +245,26 @@
             release(g - 1)
     release(count - 1)
 
-    for copy in norm_copies:
-        copy.wait_recv()
-    slab_copies = []
-    for d in range(1, n_rows):
-        copy = pltpu.make_async_remote_copy(
-            src_ref=norm_all.at[me],
-            dst_ref=norm_all.at[me],
-            send_sem=slab_send.at[d],
-            recv_sem=slab_recv.at[d],
-            device_id={"rows": lax.rem(me + d, n_rows)},
-            device_id_type=MESH,
-        )
-        copy.start()
-        slab_copies.append(copy)
-
-    cross_first, _ = split_groups(count)
-    slots = [1] * count
+    lanes = norm_all.at[0, pl.ds(0, n_width - 1)]
+    drain(lanes, norm_sem.at[1])
+    to_others(norm_all.at[me], slab_sem, "rows", me, n_rows)
+
     for item, steps in plan(count, cross_first):
         g = item[3]
         remote(item, False).wait_recv()
         for step_on in steps:
             send(step_on)
-        share_with_twin(g, rows_of(item, False), slots[g])
-        slots[g] += 1
-
-    for copy in waits:
-        copy.wait_send()
-    for copy in twins:
-        copy.wait()
-    for copy in norm_copies + sums:
-        copy.wait_send()
-    for copy in slab_copies:
-        copy.wait()
+        share_with_twin(g, rows_of(item, False))
+
+    for (link, key), rows in sent.items():
+        drain(blocks[0].at[pl.ds(0, rows), :], send_sem.at[link, key])
+    for g, block in enumerate(blocks):
+        for way in range(2):
+            drain(block.at[pl.ds(0, depth * n_rows // 2), :], twin_sem.at[way, g])
+    drain(lanes, norm_sem.at[0])
+    drain(others, sum_sem.at[0])
+    for way in range(2):
+        drain(norm_all.at[pl.ds(0, n_rows - 1)], slab_sem.at[way])
 
 
 def store(*refs):
@@ -333,27 +315,21 @@
             in_specs=[hbm] * 9,
             out_specs=[vmem] * (count + 4),
             scratch_shapes=[
-                pltpu.VMEM((count, depth, wide), jnp.float32),
-                pltpu.VMEM((count, depth, wide), jnp.float32),
+                pltpu.VMEM((count, 2, depth, wide), jnp.float32),
                 pltpu.VMEM((depth, LANES), jnp.float32),
                 pltpu.VMEM((depth,), jnp.float32),
                 pltpu.VMEM((piece,), jnp.float32),
                 pltpu.VMEM((piece,), jnp.float32),
                 pltpu.VMEM((n_rows, count, wide), jnp.float32),
-                dma((2, count)),
+                dma((count,)),
                 dma((3,)),
-                dma((n_width,)),
-                dma((n_width,)),
-                dma((n_rows,)),
-                dma((n_rows,)),
-                dma((n_rows,)),
-                dma((n_rows,)),
-                dma((2, 2, 2, count)),
+                dma((2,)),
+                dma((2,)),
+                dma((2,)),
+                dma((3, 2)),
                 dma((2, 2, 2, count)),
                 dma((5, count)),
-                dma((5, count)),
-                dma((10, count)),
-                dma((10, count)),
+                dma((2, count)),
             ],
             compiler_params=pltpu.CompilerParams(
                 collective_id=0, has_side_effects=True, vmem_limit_bytes=44 * 1024 * 1024

time: 81.3 us -> 78 us (0.959)
  Pallas kernels: 79.6 us -> 76.3 us
    pallas_call x1, Pallas kernels: 73.7 us -> 70.4 us  [shards(): pl.pallas_call(lambda *refs: kernel(n_rows, n_width, *refs), out_shape=ou...]
where the time goes in v2:
time: 78 us; the launch traced here: 77.9 us
  Pallas kernels  76.3 us (98%)
    pallas_call x1, Pallas kernels, shards(): pl.pallas_call(lambda *refs: kernel(n_rows, n_width, *refs), out_shape=ou...  70.4 us
    pallas_call x1, Pallas kernels, shards(): pl.pallas_call(store, out_shape=(jax.ShapeDtypeStruct((total, wide_query)...  5.93 us

profile of v2, /device:TPU:1, one launch (start us, length us, event | category | flops | bytes accessed | tf_op | source)
XLA Modules:
  0.0 77.9 jit_solution(9717496396564245448)
XLA Ops:
  0.6 70.4 %shard_map.144 = (bf16[7168,128]{1,0:T(8,128)(2,1)S(1)}, bf16[7168,128]{1,0:T(8,128)(2,1)S(1)}, bf16[7168,128]{1,0:T(8,128)(2,1)S(1)}, bf16[7168,128]{1,0:T(8,12...) custom-call(f32[448]{0:T(512)} %refs_0_.1, ...), custom_call_target="tpu_custom_call" | custom-call | tf_op jit(solution)/shard_map/pallas_call | solution.py:312
  71.0 5.9 %shard_map.145 = (bf16[7168,896]{1,0:T(8,128)(2,1)}, bf16[7168,128]{1,0:T(8,128)(2,1)}, bf16[7168,128]{1,0:T(8,128)(2,1)}, f32[896]{0:T(1024)}, f32[128]{0:T(128...) custom-call(bf16[7168,128]{1,0:T(8,128)(2,1)S(1)} %get-tuple-element.27.refs_0_, ...), custom_call_target="tpu_custom_call" | custom-call | tf_op jit(solution)/shard_map/pallas_call | solution.py:338
  77.0 0.2 convert_reduce_fusion
  77.2 0.7 convert_element_type.8

commit v3 on v2

--- a/solution.py
+++ b/solution.py
@@ -71,10 +71,10 @@
     *refs,
 ):
     blocks = refs[: 2 + one_query.shape[1] // one_key.shape[1]]
-    col_query, col_key, col_value, norm_all, mixed, share = refs[len(blocks) :][:6]
-    line, train, step, part, in_sem, small_sem = refs[len(blocks) + 6 :][:6]
-    norm_sem, slab_sem, sum_sem, send_sem = refs[len(blocks) + 12 :][:4]
-    ring_recv, pair_recv, twin_sem = refs[len(blocks) + 16 :]
+    col_query, col_key, col_value, serve, mixed, share = refs[len(blocks) :][:6]
+    line, train, step, part, slab, flat, in_sem, small_sem = refs[len(blocks) + 6 :][:8]
+    slab_sem, relay_send, relay_recv, sum_sem, send_sem = refs[len(blocks) + 14 :][:5]
+    ring_recv, pair_recv, twin_sem = refs[len(blocks) + 19 :]
     me = lax.axis_index("rows")
     lane = lax.axis_index("width")
     depth, wide = one_key.shape
@@ -107,14 +107,21 @@
         pl.semaphore_signal(
             barrier, inc=1, device_id={"rows": lax.rem(me + d, n_rows)}, device_id_type=MESH
         )
-    for d in range(1, n_width):
-        pl.semaphore_signal(
-            barrier, inc=1, device_id={"width": lax.rem(lane + d, n_width)}, device_id_type=MESH
-        )
+
+    envoy = me == 0
+
+    @pl.when(envoy)
+    def _():
+        for d in range(1, n_width):
+            pl.semaphore_signal(
+                barrier, inc=1, device_id={"width": lax.rem(lane + d, n_width)}, device_id_type=MESH
+            )
 
     for copy in small:
         copy.wait()
-    norm_all[me, lane] = (train[...] + step[...]).reshape(1, -1)
+    piece_size = norm_train.shape[0]
+    part[me, pl.ds(count, 1), :] = jnp.zeros((1, wide), jnp.float32)
+    part[me, pl.ds(count, 1), pl.ds(0, piece_size)] = (train[...] + step[...]).reshape(1, -1)
     for at in range(0, depth, LANES):
         size = min(LANES, depth - at)
         piece = line[pl.ds(at, size)].reshape(1, size)
@@ -134,7 +141,7 @@
         acc = lax.fori_loop(0, depth // tile, mix, jnp.zeros((8, wide), jnp.float32))
         part[me, pl.ds(g, 1), :] = jnp.sum(acc, axis=0, keepdims=True)
 
-    pl.semaphore_wait(barrier, n_rows + n_width - 2)
+    pl.semaphore_wait(barrier, n_rows - 1 + jnp.where(envoy, n_width - 1, 0))
 
     def to_others(ref, sems, axis, mine, size):
         for d in range(1, size):
@@ -148,7 +155,6 @@
             ).start()
 
     to_others(part.at[me], sum_sem, "rows", me, n_rows)
-    to_others(norm_all.at[me, lane], norm_sem, "width", lane, n_width)
 
     cross_first, _ = split_groups(count)
 
@@ -218,9 +224,9 @@
 
     others = part.at[pl.ds(0, n_rows - 1)]
     drain(others, sum_sem.at[1])
-    total = part[0]
+    total = part[0, pl.ds(0, count), :]
     for p in range(1, n_rows):
-        total = total + part[p]
+        total = total + part[p, pl.ds(0, count), :]
     scale = jnp.sqrt(total)
     inverse = 1.0 / scale
 
@@ -245,11 +251,71 @@
             release(g - 1)
     release(count - 1)
 
-    lanes = norm_all.at[0, pl.ds(0, n_width - 1)]
-    drain(lanes, norm_sem.at[1])
-    to_others(norm_all.at[me], slab_sem, "rows", me, n_rows)
-
-    for item, steps in plan(count, cross_first):
+    rows_half = n_rows // 2
+    other_slabs = slab.at[pl.ds(0, n_width - 1)]
+
+    @pl.when(envoy)
+    def _():
+        for p in range(n_rows):
+            slab[lane, pl.ds(p % 2 * rows_half + p // 2, 1), :] = part[p, pl.ds(count, 1), :]
+        to_others(slab.at[lane], slab_sem, "width", lane, n_width)
+
+    def relay(way):
+        return pltpu.make_async_remote_copy(
+            src_ref=serve,
+            dst_ref=serve,
+            send_sem=relay_send.at[way],
+            recv_sem=relay_recv.at[0],
+            device_id={"rows": target.get(way, twin)},
+            device_id_type=MESH,
+        )
+
+    def assemble():
+        drain(other_slabs, slab_sem.at[1])
+        per_line = 2 * n_width * piece_size
+        at_lane = lax.broadcasted_iota(jnp.int32, (rows_half, LANES), 1)
+        tiles = [jnp.zeros((rows_half, LANES), jnp.float32)] * (per_line // LANES)
+        for k in range(2 * n_width):
+            x = slab[k % n_width, pl.ds(k // n_width * rows_half, rows_half), :]
+            t, o = divmod(k * piece_size, LANES)
+            x = pltpu.roll(x, o, 1) if o else x
+            end = o + piece_size
+            tiles[t] = jnp.where((at_lane >= o) & (at_lane < end), x, tiles[t])
+            if end > LANES:
+                tiles[t + 1] = jnp.where(at_lane < end - LANES, x, tiles[t + 1])
+        for t, x in enumerate(tiles):
+            for a in range(rows_half):
+                flat[pl.ds(a * per_line + t * LANES, LANES)] = x[a : a + 1, :].reshape(LANES)
+        serve[...] = flat[...].astype(serve.dtype)
+
+    TWIN = 3
+    lead = core == 0
+    duties = [
+        (envoy, (UP, DOWN, ACROSS, TWIN)),
+        (lead & (place == 0) & (side == 1), (UP, DOWN, TWIN)),
+        (lead & (place == 1), (UP, TWIN)),
+        (lead & (place == 3), (TWIN,)),
+        (lead & (place == 2), (TWIN,)),
+        (core == 1, ()),
+    ]
+
+    def duty(i):
+        role, ways = duties[i]
+
+        @pl.when(role)
+        def _():
+            if i == 0:
+                assemble()
+            else:
+                drain(serve, relay_recv.at[0])
+            for way in ways:
+                relay(way).start()
+
+    schedule = plan(count, cross_first)
+    moments = [len(schedule) * (3 + i) // 12 for i in range(len(duties))]
+    for index, (item, steps) in enumerate(schedule):
+        if index in moments:
+            duty(moments.index(index))
         g = item[3]
         remote(item, False).wait_recv()
         for step_on in steps:
@@ -261,10 +327,15 @@
     for g, block in enumerate(blocks):
         for way in range(2):
             drain(block.at[pl.ds(0, depth * n_rows // 2), :], twin_sem.at[way, g])
-    drain(lanes, norm_sem.at[0])
     drain(others, sum_sem.at[0])
-    for way in range(2):
-        drain(norm_all.at[pl.ds(0, n_rows - 1)], slab_sem.at[way])
+    for i, (role, ways) in enumerate(duties):
+
+        @pl.when(role)
+        def _(i=i, ways=ways):
+            if i == 0:
+                drain(other_slabs, slab_sem.at[0])
+            for way in ways:
+                relay(way).wait_send()
 
 
 def store(*refs):
@@ -307,7 +378,7 @@
             pltpu.VMEM((wide_query,), jnp.float32),
             pltpu.VMEM((wide,), jnp.float32),
             pltpu.VMEM((wide,), jnp.float32),
-            pltpu.VMEM((n_rows, n_width, 1, piece), jnp.float32),
+            pltpu.VMEM((n_rows * n_width * piece,), jnp.bfloat16),
         )
         gathered = pl.pallas_call(
             lambda *refs: kernel(n_rows, n_width, *refs),
@@ -320,11 +391,14 @@
                 pltpu.VMEM((depth,), jnp.float32),
                 pltpu.VMEM((piece,), jnp.float32),
                 pltpu.VMEM((piece,), jnp.float32),
-                pltpu.VMEM((n_rows, count, wide), jnp.float32),
+                pltpu.VMEM((n_rows, count + 1, wide), jnp.float32),
+                pltpu.VMEM((n_width, n_rows, LANES), jnp.float32),
+                pltpu.VMEM((n_rows * n_width * piece,), jnp.float32),
                 dma((count,)),
                 dma((3,)),
                 dma((2,)),
-                dma((2,)),
+                dma((4,)),
+                dma((1,)),
                 dma((2,)),
                 dma((3, 2)),
                 dma((2, 2, 2, count)),
@@ -335,7 +409,7 @@
                 collective_id=0, has_side_effects=True, vmem_limit_bytes=44 * 1024 * 1024
             ),
         )(mix_share, norm_train, norm_step, one_query, other_query, one_key, other_key, one_value, other_value)
-        final_query, final_key, final_value, col_query, col_key, col_value, norm_all = pl.pallas_call(
+        return pl.pallas_call(
             store,
             out_shape=(
                 jax.ShapeDtypeStruct((total, wide_query), jnp.bfloat16),
@@ -348,16 +422,6 @@
             scratch_shapes=[dma((count + 4,))],
             compiler_params=pltpu.CompilerParams(vmem_limit_bytes=1024 * 1024),
         )(*gathered)
-        serve_norm = norm_all[..., 0, :].astype(jnp.bfloat16).reshape(-1)
-        return (
-            final_query,
-            final_key,
-            final_value,
-            col_query,
-            col_key,
-            col_value,
-            serve_norm,
-        )
 
     wide_spec = P("rows", "width")
     in_specs = (wide_spec,) * 6 + (P("rows"), P(("rows", "width")), P(("rows", "width")))

time: 78 us -> 75.9 us (0.973)
  Pallas kernels: 76.3 us -> 75.1 us
    pallas_call x1, Pallas kernels: 70.4 us -> 69.2 us  [shards(): pl.pallas_call(lambda *refs: kernel(n_rows, n_width, *refs), out_shape=ou...]
where the time goes in v3:
time: 75.9 us; the launch traced here: 75.8 us
  Pallas kernels  75.1 us (99%)
    pallas_call x1, Pallas kernels, shards(): pl.pallas_call(lambda *refs: kernel(n_rows, n_width, *refs), out_shape=ou...  69.2 us
    pallas_call x1, Pallas kernels, shards(): pl.pallas_call(store, out_shape=(jax.ShapeDtypeStruct((total, wide_query)...  5.94 us

profile of v3, /device:TPU:1, one launch (start us, length us, event | category | flops | bytes accessed | tf_op | source)
XLA Modules:
  0.0 75.8 jit_solution(3287548300443315900)
XLA Ops:
  0.6 69.2 %shard_map.144 = (bf16[7168,128]{1,0:T(8,128)(2,1)S(1)}, bf16[7168,128]{1,0:T(8,128)(2,1)S(1)}, bf16[7168,128]{1,0:T(8,128)(2,1)S(1)}, bf16[7168,128]{1,0:T(8,12...) custom-call(f32[448]{0:T(512)} %refs_0_.1, ...), custom_call_target="tpu_custom_call" | custom-call | tf_op jit(solution)/shard_map/pallas_call | solution.py:383
  69.8 5.9 %shard_map.145 = (bf16[7168,896]{1,0:T(8,128)(2,1)}, bf16[7168,128]{1,0:T(8,128)(2,1)}, bf16[7168,128]{1,0:T(8,128)(2,1)}, f32[896]{0:T(1024)}, f32[128]{0:T(128)}, /*index=5*/f32[128]{0:T(128)}, bf16[7168]{0:T(1024)(128)(2,1)}) custom-call(bf16[7168,128]{1,0:T(8,128)(2,1)S(1)} %get-tuple-element.20.refs_0_, ...), custom_call_target="tpu_custom_call" | custom-call | tf_op jit(solution)/shard_map/pallas_call | solution.py:412

commit v4 on v3

--- a/solution.py
+++ b/solution.py
@@ -9,6 +9,8 @@
 LANES = 128
 CIRCLE = 4
 UP, DOWN, ACROSS = 0, 1, 2
+DEPTH = 9
+LAG = 0.7
 
 
 def split_groups(count):
@@ -17,28 +19,47 @@
 
 
 def plan(count, cross_first):
-    free = [0.0, 0.0, 0.0]
-    flying = []
-
-    def send(now, item):
-        link = item[0]
-        free[link] = max(free[link], now) + (1.0 if is_whole(item) else 0.5)
-        flying.append((free[link], len(flying), item))
-
-    for g in range(count):
-        send(0.0, (UP, 0, 1, g))
-        send(0.0, (DOWN, 0, 1, g))
-        send(0.0, (ACROSS, 0, 0, g))
-    order = []
-    while flying:
-        flying.sort()
-        now, _, item = flying.pop(0)
-        now += 0.5
-        steps = followers(item, cross_first)
-        order.append((item, steps))
-        for step in steps:
-            send(now, step)
+    free, flying, ready = [0.0] * 3, [0] * 3, [[], [], []]
+    events, order, clock = [], [], [0]
+
+    def put(now, event):
+        clock[0] += 1
+        events.append((now, clock[0], event))
+
+    def offer(item):
+        clock[0] += 1
+        ready[item[0]].append((-steps_after(item, cross_first), clock[0], item))
+
+    first = [g for g in range(count) if g in cross_first]
+    second = [g for g in range(count) if g not in cross_first]
+    for k in range(max(len(first), len(second))):
+        for g in second[k : k + 1] + first[k : k + 1]:
+            put(0.05 * len(events), g)
+    while events:
+        events.sort()
+        now, _, event = events.pop(0)
+        if isinstance(event, int):
+            for item in ((ACROSS, 0, 0, event), (UP, 0, 1, event), (DOWN, 0, 1, event)):
+                offer(item)
+        else:
+            flying[event[0]] -= 1
+            for item in followers(event, cross_first):
+                offer(item)
+        sends = []
+        for link in (ACROSS, UP, DOWN):
+            ready[link].sort()
+            while ready[link] and flying[link] < DEPTH:
+                item = ready[link].pop(0)[2]
+                flying[link] += 1
+                free[link] = max(free[link], now) + (1.0 if is_whole(item) else 0.5)
+                put(free[link] + LAG, item)
+                sends.append(item)
+        order.append((event, sends))
     return order
+
+
+def steps_after(item, cross_first):
+    return max([1 + steps_after(x, cross_first) for x in followers(item, cross_first)], default=0)
 
 
 def is_whole(item):
@@ -230,13 +251,8 @@
     scale = jnp.sqrt(total)
     inverse = 1.0 / scale
 
-    def release(g):
-        send((ACROSS, 0, 0, g))
-        send((UP, 0, 1, g))
-        send((DOWN, 0, 1, g))
-        share_with_twin(g, whole(me))
-
-    for g, (_, _, out, col, at) in enumerate(groups):
+    def make_block(g):
+        _, _, out, col, at = groups[g]
         col[pl.ds(at, wide)] = scale[g : g + 1, :].reshape(wide)
         by = inverse[g : g + 1, :]
 
@@ -247,15 +263,11 @@
             return carry
 
         lax.fori_loop(0, depth // tile, narrow, 0)
-        if g:
-            release(g - 1)
-    release(count - 1)
 
     rows_half = n_rows // 2
     other_slabs = slab.at[pl.ds(0, n_width - 1)]
 
-    @pl.when(envoy)
-    def _():
+    def meet():
         for p in range(n_rows):
             slab[lane, pl.ds(p % 2 * rows_half + p // 2, 1), :] = part[p, pl.ds(count, 1), :]
         to_others(slab.at[lane], slab_sem, "width", lane, n_width)
@@ -313,14 +325,20 @@
 
     schedule = plan(count, cross_first)
     moments = [len(schedule) * (3 + i) // 12 for i in range(len(duties))]
-    for index, (item, steps) in enumerate(schedule):
+    for index, (event, items) in enumerate(schedule):
+        if index == count:
+            pl.when(envoy)(meet)
         if index in moments:
             duty(moments.index(index))
-        g = item[3]
-        remote(item, False).wait_recv()
-        for step_on in steps:
-            send(step_on)
-        share_with_twin(g, rows_of(item, False))
+        if isinstance(event, int):
+            make_block(event)
+            g, rows = event, whole(me)
+        else:
+            remote(event, False).wait_recv()
+            g, rows = event[3], rows_of(event, False)
+        for item in items:
+            send(item)
+        share_with_twin(g, rows)
 
     for (link, key), rows in sent.items():
         drain(blocks[0].at[pl.ds(0, rows), :], send_sem.at[link, key])

time: 75.9 us -> 74.6 us (0.983)
  Pallas kernels: 75.1 us -> 73.8 us
    pallas_call x1, Pallas kernels: 69.2 us -> 67.9 us  [shards(): pl.pallas_call(lambda *refs: kernel(n_rows, n_width, *refs), out_shape=ou...]
where the time goes in v4:
time: 74.6 us; the launch traced here: 74.4 us
  Pallas kernels  73.8 us (99%)
    pallas_call x1, Pallas kernels, shards(): pl.pallas_call(lambda *refs: kernel(n_rows, n_width, *refs), out_shape=ou...  67.9 us
    pallas_call x1, Pallas kernels, shards(): pl.pallas_call(store, out_shape=(jax.ShapeDtypeStruct((total, wide_query)...  5.94 us

profile of v4, /device:TPU:1, one launch (start us, length us, event | category | flops | bytes accessed | tf_op | source)
XLA Modules:
  0.0 74.4 jit_solution(4778153801039995494)
XLA Ops:
  0.6 67.9 %shard_map.144 = (bf16[7168,128]{1,0:T(8,128)(2,1)S(1)}, bf16[7168,128]{1,0:T(8,128)(2,1)S(1)}, bf16[7168,128]{1,0:T(8,128)(2,1)S(1)}, bf16[7168,128]{1,0:T(8,12...) custom-call(f32[448]{0:T(512)} %refs_0_.1, ...), custom_call_target="tpu_custom_call" | custom-call | tf_op jit(solution)/shard_map/pallas_call | solution.py:401
  68.5 5.9 %shard_map.145 = (bf16[7168,896]{1,0:T(8,128)(2,1)}, bf16[7168,128]{1,0:T(8,128)(2,1)}, bf16[7168,128]{1,0:T(8,128)(2,1)}, f32[896]{0:T(1024)}, f32[128]{0:T(128)}, /*index=5*/f32[128]{0:T(128)}, bf16[7168]{0:T(1024)(128)(2,1)}) custom-call(bf16[7168,128]{1,0:T(8,128)(2,1)S(1)} %get-tuple-element.20.refs_0_, ...), custom_call_target="tpu_custom_call" | custom-call | tf_op jit(solution)/shard_map/pallas_call | solution.py:430

commit v5 on v4

v5 whole, which is shorter than its diff:
```python
import jax
import jax.numpy as jnp
from jax import lax
from jax.experimental import pallas as pl
from jax.experimental.pallas import tpu as pltpu
from jax.sharding import PartitionSpec as P

MESH = pl.DeviceIdType.MESH
LANES = 128
CIRCLE = 4
UP, DOWN, ACROSS = 0, 1, 2
SPAN = 2
WINDOW = 4
DEPTH = 9
LAG = 0.7


def layout(count):
    first = (5 * count + 4) // 9

    def cut(start, end):
        return [list(range(i, min(i + SPAN, end))) for i in range(start, end, SPAN)]

    blocks = cut(0, first) + cut(first, count)
    return blocks, [b for b, pieces in enumerate(blocks) if pieces[0] < first]


def plan(weights, cross_first):
    free, flying, ready = [0.0] * 3, [0] * 3, [[], [], []]
    events, order, clock = [], [], [0]

    def put(now, event):
        clock[0] += 1
        events.append((now, clock[0], event))

    def offer(item):
        clock[0] += 1
        ready[item[0]].append((-steps_after(item, cross_first), clock[0], item))

    first = cross_first
    second = [b for b in range(len(weights)) if b not in cross_first]
    for k in range(max(len(first), len(second))):
        for b in second[k : k + 1] + first[k : k + 1]:
            put(0.1 * len(events), b)
    while events:
        events.sort()
        now, _, event = events.pop(0)
        if isinstance(event, int):
            for item in ((ACROSS, 0, 0, event), (UP, 0, 1, event), (DOWN, 0, 1, event)):
                offer(item)
        else:
            flying[event[0]] -= 1
            for item in followers(event, cross_first):
                offer(item)
        sends = []
        for link in (ACROSS, UP, DOWN):
            ready[link].sort()
            while ready[link] and flying[link] < DEPTH:
                item = ready[link].pop(0)[2]
                flying[link] += 1
                size = weights[item[3]] * (1.0 if is_whole(item) else 0.5)
                free[link] = max(free[link], now) + size
                put(free[link] + LAG, item)
                sends.append(item)
        order.append((event, sends))
    return order


def steps_after(item, cross_first):
    return max([1 + steps_after(x, cross_first) for x in followers(item, cross_first)], default=0)


def is_whole(item):
    link, _, hop, _ = item
    return hop < 3 if link == ACROSS else hop == 1


def followers(item, cross_first):
    link, far, hop, g = item
    if link == ACROSS:
        return [(UP, 1, 1, g), (DOWN, 1, 1, g)] if g in cross_first else []
    steps = [(link, far, 2, g)] if hop == 1 else []
    if g not in cross_first:
        steps.append((ACROSS, 0, 1 + link if hop == 1 else 3 + link, g))
    return steps


def kernel(
    n_rows,
    n_width,
    pieces_of,
    cross_first,
    share_in,
    norm_train,
    norm_step,
    one_query,
    other_query,
    one_key,
    other_key,
    one_value,
    other_value,
    *refs,
):
    blocks = refs[: len(pieces_of)]
    col_query, col_key, col_value, serve, mixed, share = refs[len(blocks) :][:6]
    line, train, step, early_part, part, slab, flat = refs[len(blocks) + 6 :][:7]
    in_sem, small_sem, slab_sem, relay_send, relay_recv = refs[len(blocks) + 13 :][:5]
    early_sem, sum_sem, send_sem, ring_recv, pair_recv, twin_sem = refs[len(blocks) + 18 :]
    me = lax.axis_index("rows")
    lane = lax.axis_index("width")
    depth, wide = one_key.shape
    groups = [
        (one_key, other_key, col_key, 0),
        (one_value, other_value, col_value, 0),
    ] + [
        (one_query, other_query, col_query, j * wide)
        for j in range(one_query.shape[1] // wide)
    ]
    count = len(groups)
    tile = 64 if depth % 64 == 0 else 16
    half = depth // 2

    def drain(ref, sem):
        pltpu.make_async_copy(ref, ref, sem).wait()

    small = []
    for i, (src, dst) in enumerate(((share_in, line), (norm_train, train), (norm_step, step))):
        small.append(pltpu.make_async_copy(src, dst, small_sem.at[i]))
        small[-1].start()

    kinds = [cross_first, [b for b in range(len(blocks)) if b not in cross_first]]
    early = [p for kind in kinds for p in pieces_of[kind[0]]]
    late = [p for p in range(count) if p not in early]
    loading = early + late
    parts = {p: (early_part, k) for k, p in enumerate(early)}
    parts.update({p: (part, k) for k, p in enumerate(late)})

    def load(p):
        one, other, _, at = groups[p]
        for i, src in enumerate((one, other)):
            src = src.at[:, pl.ds(at, wide)]
            pltpu.make_async_copy(src, mixed.at[p, i], in_sem.at[p]).start()

    for p in loading[:WINDOW]:
        load(p)

    barrier = pltpu.get_barrier_semaphore()
    for d in range(1, n_rows):
        pl.semaphore_signal(
            barrier, inc=1, device_id={"rows": lax.rem(me + d, n_rows)}, device_id_type=MESH
        )

    envoy = me == 0
    row = n_width // 2
    along = [lane // row * row + (lane + d) % row for d in range(1, row)]
    opposite = (lane + row) % n_width

    @pl.when(envoy)
    def _():
        for peer in along + [opposite]:
            pl.semaphore_signal(barrier, inc=1, device_id={"width": peer}, device_id_type=MESH)

    for copy in small:
        copy.wait()
    piece_size = norm_train.shape[0]
    norm_at = pl.ds(len(late), 1)
    part[me, norm_at, :] = jnp.zeros((1, wide), jnp.float32)
    part[me, norm_at, pl.ds(0, piece_size)] = (train[...] + step[...]).reshape(1, -1)
    for at in range(0, depth, LANES):
        size = min(LANES, depth - at)
        piece = line[pl.ds(at, size)].reshape(1, size)
        share[pl.ds(at, size), :] = jnp.broadcast_to(piece, (LANES, size)).T

    core = me % 2
    place = (me // 2) % CIRCLE
    side = me // (2 * CIRCLE)

    def device(sides, steps, cores=0):
        chip = (side + sides) % 2 * CIRCLE + (place + steps + CIRCLE) % CIRCLE
        return chip * 2 + (core + cores) % 2

    far = [(a, b, c) for b in (2, 1, -1, 0) for a in (1, 0) for c in (1, 0) if (a, b, c) != (0, 0, 0)]

    def sum_up(p):
        drain(mixed.at[p], in_sem.at[p])
        if loading.index(p) + WINDOW < count:
            load(loading[loading.index(p) + WINDOW])

        def mix(i, acc):
            rows = pl.ds(pl.multiple_of(i * tile, tile), tile)
            s = share[rows, :]
            s = jnp.concatenate([s] * (wide // LANES), axis=1)
            r = s * mixed[p, 0, rows, :] + (1.0 - s) * mixed[p, 1, rows, :]
            mixed[p, 0, rows, :] = r
            return acc + jnp.sum((r * r).reshape(tile // 8, 8, wide), axis=0)

        acc = lax.fori_loop(0, depth // tile, mix, jnp.zeros((8, wide), jnp.float32))
        into, at_row = parts[p]
        into[me, pl.ds(at_row, 1), :] = jnp.sum(acc, axis=0, keepdims=True)

    def to_group(ref, sems):
        for where in far:
            pltpu.make_async_remote_copy(
                src_ref=ref.at[me],
                dst_ref=ref.at[me],
                send_sem=sems.at[0],
                recv_sem=sems.at[1],
                device_id={"rows": device(*where)},
                device_id_type=MESH,
            ).start()

    for p in early:
        sum_up(p)
    pl.semaphore_wait(barrier, n_rows - 1 + jnp.where(envoy, row, 0))
    to_group(early_part, early_sem)
    for p in late:
        sum_up(p)
    to_group(part, sum_sem)

    twin = me + 1 - 2 * core
    target = {UP: device(0, 1), DOWN: device(0, -1), ACROSS: device(1, 0)}
    def whole(owner):
        return pl.ds(pl.multiple_of(owner * depth, half), depth)

    def part_of(owner, way):
        return pl.ds(pl.multiple_of(owner * depth + way * half, half), half)

    def rows_of(item, sender):
        link, far, hop, _ = item
        if link == ACROSS:
            side_of = 0 if sender else 1
            if hop >= 3:
                return part_of(device(side_of, 2), hop - 3)
            return whole(device(side_of, (0, -1, 1)[hop]))
        away = hop - 1 if sender else hop
        owner = device(far, -away if link == UP else away)
        return whole(owner) if hop == 1 else part_of(owner, link)

    def remote(item, sender):
        link, far, hop, g = item
        ref = blocks[g].at[rows_of(item, sender), :]
        if link == ACROSS:
            arrived = pair_recv.at[hop, g]
        else:
            arrived = ring_recv.at[link, far, hop - 1, g]
        return pltpu.make_async_remote_copy(
            src_ref=ref,
            dst_ref=ref,
            send_sem=send_sem.at[link, g],
            recv_sem=arrived,
            device_id={"rows": target[link]},
            device_id_type=MESH,
        )

    sent = {}

    def send(item):
        remote(item, True).start()
        key = item[0], item[3]
        sent[key] = sent.get(key, 0) + (depth if is_whole(item) else half)

    def share_with_twin(g, rows):
        ref = blocks[g].at[rows, :]
        pltpu.make_async_remote_copy(
            src_ref=ref,
            dst_ref=ref,
            send_sem=twin_sem.at[0, g],
            recv_sem=twin_sem.at[1, g],
            device_id={"rows": twin},
            device_id_type=MESH,
        ).start()

    def scales(ref, sems, size):
        drain(ref.at[pl.ds(0, n_rows - 1)], sems.at[1])
        total = ref[0, pl.ds(0, size), :]
        for d in range(1, n_rows):
            total = total + ref[d, pl.ds(0, size), :]
        scale = jnp.sqrt(total)
        return scale, 1.0 / scale

    early_scales = scales(early_part, early_sem, len(early))
    late_scales = None

    def make_block(g):
        pieces, out = pieces_of[g], blocks[g]
        scale, inverse = early_scales if pieces[0] in early else late_scales
        for p in pieces:
            _, _, col, at = groups[p]
            at_row = parts[p][1]
            col[pl.ds(at, wide)] = scale[at_row : at_row + 1, :].reshape(wide)

        def narrow(i, carry):
            rows = pl.ds(pl.multiple_of(i * tile, tile), tile)
            here = pl.ds(pl.multiple_of(me * depth + i * tile, tile), tile)
            for j, p in enumerate(pieces):
                at_row = parts[p][1]
                made = mixed[p, 0, rows, :] * inverse[at_row : at_row + 1, :]
                out[here, pl.ds(j * wide, wide)] = made.astype(out.dtype)
            return carry

        lax.fori_loop(0, depth // tile, narrow, 0)

    rows_half = n_rows // 2

    def meet():
        for d in range(n_rows):
            slab[lane, pl.ds(d % 2 * rows_half + d // 2, 1), :] = part[d, norm_at, :]
        for peer in along:
            pltpu.make_async_remote_copy(
                src_ref=slab.at[lane],
                dst_ref=slab.at[lane],
                send_sem=slab_sem.at[0, 0],
                recv_sem=slab_sem.at[0, 1],
                device_id={"width": peer},
                device_id_type=MESH,
            ).start()

    def swap():
        drain(slab.at[pl.ds(0, row - 1)], slab_sem.at[0, 1])
        mine = slab.at[pl.ds(lane // row * row, row)]
        pltpu.make_async_remote_copy(
            src_ref=mine,
            dst_ref=mine,
            send_sem=slab_sem.at[1, 0],
            recv_sem=slab_sem.at[1, 1],
            device_id={"width": opposite},
            device_id_type=MESH,
        ).start()

    def relay(way):
        return pltpu.make_async_remote_copy(
            src_ref=serve,
            dst_ref=serve,
            send_sem=relay_send.at[way],
            recv_sem=relay_recv.at[0],
            device_id={"rows": target.get(way, twin)},
            device_id_type=MESH,
        )

    def assemble():
        drain(slab.at[pl.ds(0, row)], slab_sem.at[1, 1])
        per_line = 2 * n_width * piece_size
        at_lane = lax.broadcasted_iota(jnp.int32, (rows_half, LANES), 1)
        tiles = [jnp.zeros((rows_half, LANES), jnp.float32)] * (per_line // LANES)
        for k in range(2 * n_width):
            x = slab[k % n_width, pl.ds(k // n_width * rows_half, rows_half), :]
            t, o = divmod(k * piece_size, LANES)
            x = pltpu.roll(x, o, 1) if o else x
            end = o + piece_size
            tiles[t] = jnp.where((at_lane >= o) & (at_lane < end), x, tiles[t])
            if end > LANES:
                tiles[t + 1] = jnp.where(at_lane < end - LANES, x, tiles[t + 1])
        for t, x in enumerate(tiles):
            for a in range(rows_half):
                flat[pl.ds(a * per_line + t * LANES, LANES)] = x[a : a + 1, :].reshape(LANES)
        serve[...] = flat[...].astype(serve.dtype)

    TWIN = 3
    lead = core == 0
    duties = [
        (envoy, (UP, DOWN, ACROSS, TWIN)),
        (lead & (place == 0) & (side == 1), (UP, DOWN, TWIN)),
        (lead & (place == 1), (UP, TWIN)),
        (lead & (place == 3), (TWIN,)),
        (lead & (place == 2), (TWIN,)),
        (core == 1, ()),
    ]

    def duty(i):
        role, ways = duties[i]

        @pl.when(role)
        def _():
            if i == 0:
                assemble()
            else:
                drain(serve, relay_recv.at[0])
            for way in ways:
                relay(way).start()

    schedule = plan([len(pieces) for pieces in pieces_of], cross_first)
    moments = [len(schedule) * (3 + i) // 12 for i in range(len(duties))]
    meeting, swapping = len(blocks), (len(blocks) + moments[0]) // 2
    for index, (event, items) in enumerate(schedule):
        if index == meeting:
            pl.when(envoy)(meet)
        if index == swapping:
            pl.when(envoy)(swap)
        if index in moments:
            duty(moments.index(index))
        if isinstance(event, int):
            if late_scales is None and pieces_of[event][0] in late:
                late_scales = scales(part, sum_sem, len(late))
            make_block(event)
            g, rows = event, whole(me)
        else:
            remote(event, False).wait_recv()
            g, rows = event[3], rows_of(event, False)
        for item in items:
            send(item)
        share_with_twin(g, rows)

    for (link, key), rows in sent.items():
        drain(blocks[key].at[pl.ds(0, rows), :], send_sem.at[link, key])
    for g, block in enumerate(blocks):
        for way in range(2):
            drain(block.at[pl.ds(0, depth * n_rows // 2), :], twin_sem.at[way, g])
    drain(early_part.at[pl.ds(0, n_rows - 1)], early_sem.at[0])
    drain(part.at[pl.ds(0, n_rows - 1)], sum_sem.at[0])
    for i, (role, ways) in enumerate(duties):

        @pl.when(role)
        def _(i=i, ways=ways):
            if i == 0:
                drain(slab.at[pl.ds(0, row - 1)], slab_sem.at[0, 0])
                drain(slab.at[pl.ds(0, row)], slab_sem.at[1, 0])
            for way in ways:
                relay(way).wait_send()


def store(pieces_of, wide, *refs):
    outs, sem = refs[-8:-1], refs[-1]
    blocks, small = refs[:-12], refs[-12:-8]
    pairs = list(zip(small, outs[3:]))
    for pieces, block in zip(pieces_of, blocks):
        lone = [p for p in pieces if p < 2]
        for j, p in enumerate(lone):
            pairs.append((block.at[:, pl.ds(j * wide, wide)], outs[1 + p]))
        if pieces[len(lone) :]:
            at, size = (pieces[len(lone)] - 2) * wide, (len(pieces) - len(lone)) * wide
            pairs.append((block.at[:, pl.ds(len(lone) * wide, size)], outs[0].at[:, pl.ds(at, size)]))
    copies = [pltpu.make_async_copy(src, dst, sem.at[i]) for i, (src, dst) in enumerate(pairs)]
    for copy in copies:
        copy.start()
    for copy in copies:
        copy.wait()


def solution(mesh):
    n_rows, n_width = mesh.shape["rows"], mesh.shape["width"]

    def shards(
        one_query,
        other_query,
        one_key,
        other_key,
        one_value,
        other_value,
        mix_share,
        norm_train,
        norm_step,
    ):
        depth, wide = one_key.shape
        wide_query = one_query.shape[1]
        count = 2 + wide_query // wide
        pieces_of, cross_first = layout(count)
        n_blocks = len(pieces_of)
        n_early = len(pieces_of[0]) + len(pieces_of[len(cross_first)])
        piece = norm_train.shape[0]
        total = depth * n_rows
        hbm = pl.BlockSpec(memory_space=pltpu.HBM)
        vmem = pl.BlockSpec(memory_space=pltpu.VMEM)
        dma = pltpu.SemaphoreType.DMA
        out_shape = tuple(
            pltpu.VMEM((total, wide * len(pieces)), jnp.bfloat16) for pieces in pieces_of
        ) + (
            pltpu.VMEM((wide_query,), jnp.float32),
            pltpu.VMEM((wide,), jnp.float32),
            pltpu.VMEM((wide,), jnp.float32),
            pltpu.VMEM((n_rows * n_width * piece,), jnp.bfloat16),
        )
        gathered = pl.pallas_call(
            lambda *refs: kernel(n_rows, n_width, pieces_of, cross_first, *refs),
            out_shape=out_shape,
            in_specs=[hbm] * 9,
            out_specs=[vmem] * (n_blocks + 4),
            scratch_shapes=[
                pltpu.VMEM((count, 2, depth, wide), jnp.float32),
                pltpu.VMEM((depth, LANES), jnp.float32),
                pltpu.VMEM((depth,), jnp.float32),
                pltpu.VMEM((piece,), jnp.float32),
                pltpu.VMEM((piece,), jnp.float32),
                pltpu.VMEM((n_rows, n_early, wide), jnp.float32),
                pltpu.VMEM((n_rows, count - n_early + 1, wide), jnp.float32),
                pltpu.VMEM((n_width, n_rows, LANES), jnp.float32),
                pltpu.VMEM((n_rows * n_width * piece,), jnp.float32),
                dma((count,)),
                dma((3,)),
                dma((2, 2)),
                dma((4,)),
                dma((1,)),
                dma((2,)),
                dma((2,)),
                dma((3, n_blocks)),
                dma((2, 2, 2, n_blocks)),
                dma((5, n_blocks)),
                dma((2, n_blocks)),
            ],
            compiler_params=pltpu.CompilerParams(
                collective_id=0, has_side_effects=True, vmem_limit_bytes=44 * 1024 * 1024
            ),
        )(mix_share, norm_train, norm_step, one_query, other_query, one_key, other_key, one_value, other_value)
        return pl.pallas_call(
            lambda *refs: store(pieces_of, wide, *refs),
            out_shape=(
                jax.ShapeDtypeStruct((total, wide_query), jnp.bfloat16),
                jax.ShapeDtypeStruct((total, wide), jnp.bfloat16),
                jax.ShapeDtypeStruct((total, wide), jnp.bfloat16),
            )
            + tuple(jax.ShapeDtypeStruct(o.shape, o.dtype) for o in out_shape[n_blocks:]),
            in_specs=[vmem] * (n_blocks + 4),
            out_specs=[hbm] * 7,
            scratch_shapes=[dma((count + 4,))],
            compiler_params=pltpu.CompilerParams(vmem_limit_bytes=1024 * 1024),
        )(*gathered)

    wide_spec = P("rows", "width")
    in_specs = (wide_spec,) * 6 + (P("rows"), P(("rows", "width")), P(("rows", "width")))
    out_specs = (P(None, "width"),) * 3 + (P("width"),) * 3 + (P(),)
    return jax.shard_map(shards, mesh=mesh, in_specs=in_specs, out_specs=out_specs, check_vma=False)
```

time: 74.6 us -> 72.5 us (0.972)
  Pallas kernels: 73.8 us -> 71.7 us
    pallas_call x2, Pallas kernels: 73.8 us -> 71.7 us  [the longest x1 65.7 us: shards(): pl.pallas_call(lambda *refs: kernel(n_rows, n_width, pieces_of, cross_fir...]
where the time goes in v5:
time: 72.5 us; the launch traced here: 72.3 us
  Pallas kernels  71.7 us (99%)
    pallas_call x1, Pallas kernels, shards(): pl.pallas_call(lambda *refs: kernel(n_rows, n_width, pieces_of, cross_fir...  65.7 us
    pallas_call x1, Pallas kernels, shards(): pl.pallas_call(lambda *refs: store(pieces_of, wide, *refs), out_shape=(ja...  6.04 us

profile of v5, /device:TPU:1, one launch (start us, length us, event | category | flops | bytes accessed | tf_op | source)
XLA Modules:
  0.0 72.3 jit_solution(665230097924742596)
XLA Ops:
  0.6 65.7 %shard_map.144 = (bf16[7168,256]{1,0:T(8,128)(2,1)S(1)}, bf16[7168,256]{1,0:T(8,128)(2,1)S(1)}, bf16[7168,128]{1,0:T(8,128)(2,1)S(1)}, bf16[7168,256]{1,0:T(8,12...) custom-call(f32[448]{0:T(512)} %refs_0_.1, ...), custom_call_target="tpu_custom_call" | custom-call | tf_op jit(solution)/shard_map/pallas_call | solution.py:472
  66.3 6.0 %shard_map.145 = (bf16[7168,896]{1,0:T(8,128)(2,1)}, bf16[7168,128]{1,0:T(8,128)(2,1)}, bf16[7168,128]{1,0:T(8,128)(2,1)}, f32[896]{0:T(1024)}, f32[128]{0:T(128)}, /*index=5*/f32[128]{0:T(128)}, bf16[7168]{0:T(1024)(128)(2,1)}) custom-call(bf16[7168,256]{1,0:T(8,128)(2,1)S(1)} %get-tuple-element.16.refs_0_, ...), custom_call_target="tpu_custom_call" | custom-call | tf_op jit(solution)/shard_map/pallas_call | solution.py:503

commit v6 on v5

--- a/solution.py
+++ b/solution.py
@@ -25,7 +25,12 @@
     return blocks, [b for b, pieces in enumerate(blocks) if pieces[0] < first]
 
 
-def plan(weights, cross_first):
+def ahead_of(blocks, cross_first):
+    last = cross_first[-1]
+    return {(UP, 0, 1, last): 0, (DOWN, 0, 1, last): 1, (ACROSS, 0, 0, last): 0}
+
+
+def plan(weights, cross_first, ahead):
     free, flying, ready = [0.0] * 3, [0] * 3, [[], [], []]
     events, order, clock = [], [], [0]
 
@@ -58,7 +63,7 @@
             while ready[link] and flying[link] < DEPTH:
                 item = ready[link].pop(0)[2]
                 flying[link] += 1
-                size = weights[item[3]] * (1.0 if is_whole(item) else 0.5)
+                size = weights[item[3]] * (1.0 if is_whole(item) and item not in ahead else 0.5)
                 free[link] = max(free[link], now) + size
                 put(free[link] + LAG, item)
                 sends.append(item)
@@ -90,6 +95,8 @@
     n_width,
     pieces_of,
     cross_first,
+    ahead,
+    schedule,
     share_in,
     norm_train,
     norm_step,
@@ -105,7 +112,8 @@
     col_query, col_key, col_value, serve, mixed, share = refs[len(blocks) :][:6]
     line, train, step, early_part, part, slab, flat = refs[len(blocks) + 6 :][:7]
     in_sem, small_sem, slab_sem, relay_send, relay_recv = refs[len(blocks) + 13 :][:5]
-    early_sem, sum_sem, send_sem, ring_recv, pair_recv, twin_sem = refs[len(blocks) + 18 :]
+    early_sem, sum_sem, send_sem, recv_sem, twin_sem = refs[len(blocks) + 18 :][:5]
+    stage, stage_sem = refs[len(blocks) + 23 :]
     me = lax.axis_index("rows")
     lane = lax.axis_index("width")
     depth, wide = one_key.shape
@@ -119,6 +127,7 @@
     count = len(groups)
     tile = 64 if depth % 64 == 0 else 16
     half = depth // 2
+    step_rows = 32 if half % 32 == 0 else 16
 
     def drain(ref, sem):
         pltpu.make_async_copy(ref, ref, sem).wait()
@@ -130,7 +139,8 @@
 
     kinds = [cross_first, [b for b in range(len(blocks)) if b not in cross_first]]
     early = [p for kind in kinds for p in pieces_of[kind[0]]]
-    late = [p for p in range(count) if p not in early]
+    (first_out,) = pieces_of[cross_first[-1]]
+    late = [first_out] + [p for p in range(count) if p not in early + [first_out]]
     loading = early + late
     parts = {p: (early_part, k) for k, p in enumerate(early)}
     parts.update({p: (part, k) for k, p in enumerate(late)})
@@ -213,41 +223,59 @@
         sum_up(p)
     pl.semaphore_wait(barrier, n_rows - 1 + jnp.where(envoy, row, 0))
     to_group(early_part, early_sem)
-    for p in late:
+    twin = me + 1 - 2 * core
+    target = {UP: device(0, 1), DOWN: device(0, -1), ACROSS: device(1, 0)}
+    sum_up(first_out)
+    for item, way in ahead.items():
+        pltpu.make_async_remote_copy(
+            src_ref=mixed.at[first_out, 0, pl.ds(way * half, half), :],
+            dst_ref=stage.at[item[0]],
+            send_sem=stage_sem.at[0, item[0]],
+            recv_sem=stage_sem.at[1, item[0]],
+            device_id={"rows": target[item[0]]},
+            device_id_type=MESH,
+        ).start()
+    for p in late[1:]:
         sum_up(p)
     to_group(part, sum_sem)
 
-    twin = me + 1 - 2 * core
-    target = {UP: device(0, 1), DOWN: device(0, -1), ACROSS: device(1, 0)}
+    slots = {}
+    for event, _ in schedule:
+        if not isinstance(event, int):
+            slots[event] = len(slots)
+
+    def size_of(item):
+        return depth if is_whole(item) and item not in ahead else half
+
     def whole(owner):
         return pl.ds(pl.multiple_of(owner * depth, half), depth)
 
     def part_of(owner, way):
         return pl.ds(pl.multiple_of(owner * depth + way * half, half), half)
 
-    def rows_of(item, sender):
+    def held(item, sender):
         link, far, hop, _ = item
         if link == ACROSS:
             side_of = 0 if sender else 1
-            if hop >= 3:
-                return part_of(device(side_of, 2), hop - 3)
-            return whole(device(side_of, (0, -1, 1)[hop]))
+            owner = device(side_of, (0, -1, 1, 2, 2)[hop])
+            return owner, None if hop < 3 else hop - 3
         away = hop - 1 if sender else hop
-        owner = device(far, -away if link == UP else away)
-        return whole(owner) if hop == 1 else part_of(owner, link)
+        return device(far, -away if link == UP else away), None if hop == 1 else link
+
+    def rows_of(item, sender):
+        owner, way = held(item, sender)
+        if item in ahead:
+            way = 1 - ahead[item]
+        return whole(owner) if way is None else part_of(owner, way)
 
     def remote(item, sender):
-        link, far, hop, g = item
+        link, _, _, g = item
         ref = blocks[g].at[rows_of(item, sender), :]
-        if link == ACROSS:
-            arrived = pair_recv.at[hop, g]
-        else:
-            arrived = ring_recv.at[link, far, hop - 1, g]
         return pltpu.make_async_remote_copy(
             src_ref=ref,
             dst_ref=ref,
-            send_sem=send_sem.at[link, g],
-            recv_sem=arrived,
+            send_sem=send_sem.at[link],
+            recv_sem=recv_sem.at[slots[item]],
             device_id={"rows": target[link]},
             device_id_type=MESH,
         )
@@ -256,16 +284,15 @@
 
     def send(item):
         remote(item, True).start()
-        key = item[0], item[3]
-        sent[key] = sent.get(key, 0) + (depth if is_whole(item) else half)
+        sent[item[0]] = sent.get(item[0], 0) + size_of(item) * len(pieces_of[item[3]])
 
     def share_with_twin(g, rows):
         ref = blocks[g].at[rows, :]
         pltpu.make_async_remote_copy(
             src_ref=ref,
             dst_ref=ref,
-            send_sem=twin_sem.at[0, g],
-            recv_sem=twin_sem.at[1, g],
+            send_sem=twin_sem.at[0, g // 2],
+            recv_sem=twin_sem.at[1, g // 2],
             device_id={"rows": twin},
             device_id_type=MESH,
         ).start()
@@ -280,6 +307,20 @@
 
     early_scales = scales(early_part, early_sem, len(early))
     late_scales = None
+
+    def take_in(item):
+        link, _, _, g = item
+        drain(stage.at[link], stage_sem.at[1, link])
+        start = held(item, False)[0] * depth + ahead[item] * half
+        by = late_scales[1][:1, :]
+
+        def narrow(i, carry):
+            rows = pl.ds(pl.multiple_of(i * step_rows, step_rows), step_rows)
+            here = pl.ds(pl.multiple_of(start + i * step_rows, step_rows), step_rows)
+            blocks[g][here, :] = (stage[link, rows, :] * by).astype(blocks[g].dtype)
+            return carry
+
+        lax.fori_loop(0, half // step_rows, narrow, 0)
 
     def make_block(g):
         pieces, out = pieces_of[g], blocks[g]
@@ -378,7 +419,6 @@
             for way in ways:
                 relay(way).start()
 
-    schedule = plan([len(pieces) for pieces in pieces_of], cross_first)
     moments = [len(schedule) * (3 + i) // 12 for i in range(len(duties))]
     meeting, swapping = len(blocks), (len(blocks) + moments[0]) // 2
     for index, (event, items) in enumerate(schedule):
@@ -394,17 +434,26 @@
             make_block(event)
             g, rows = event, whole(me)
         else:
+            if event in ahead:
+                take_in(event)
             remote(event, False).wait_recv()
-            g, rows = event[3], rows_of(event, False)
+            g = event[3]
+            rows = whole(held(event, False)[0]) if event in ahead else rows_of(event, False)
         for item in items:
             send(item)
         share_with_twin(g, rows)
 
-    for (link, key), rows in sent.items():
-        drain(blocks[key].at[pl.ds(0, rows), :], send_sem.at[link, key])
-    for g, block in enumerate(blocks):
+    def drain_rows(rows, sem):
+        drain(blocks[0].at[pl.ds(0, rows // len(pieces_of[0])), :], sem)
+
+    for item in ahead:
+        drain(stage.at[item[0]], stage_sem.at[0, item[0]])
+    for link, rows in sent.items():
+        drain_rows(rows, send_sem.at[link])
+    for g in range(0, len(blocks), 2):
         for way in range(2):
-            drain(block.at[pl.ds(0, depth * n_rows // 2), :], twin_sem.at[way, g])
+            rows = depth * n_rows // 2 * sum(len(pieces) for pieces in pieces_of[g : g + 2])
+            drain_rows(rows, twin_sem.at[way, g // 2])
     drain(early_part.at[pl.ds(0, n_rows - 1)], early_sem.at[0])
     drain(part.at[pl.ds(0, n_rows - 1)], sum_sem.at[0])
     for i, (role, ways) in enumerate(duties):
@@ -455,6 +504,9 @@
         count = 2 + wide_query // wide
         pieces_of, cross_first = layout(count)
         n_blocks = len(pieces_of)
+        ahead = ahead_of(pieces_of, cross_first)
+        schedule = plan([len(pieces) for pieces in pieces_of], cross_first, ahead)
+        n_items = len(schedule) - n_blocks
         n_early = len(pieces_of[0]) + len(pieces_of[len(cross_first)])
         piece = norm_train.shape[0]
         total = depth * n_rows
@@ -470,7 +522,7 @@
             pltpu.VMEM((n_rows * n_width * piece,), jnp.bfloat16),
         )
         gathered = pl.pallas_call(
-            lambda *refs: kernel(n_rows, n_width, pieces_of, cross_first, *refs),
+            lambda *refs: kernel(n_rows, n_width, pieces_of, cross_first, ahead, schedule, *refs),
             out_shape=out_shape,
             in_specs=[hbm] * 9,
             out_specs=[vmem] * (n_blocks + 4),
@@ -491,10 +543,11 @@
                 dma((1,)),
                 dma((2,)),
                 dma((2,)),
-                dma((3, n_blocks)),
-                dma((2, 2, 2, n_blocks)),
-                dma((5, n_blocks)),
-                dma((2, n_blocks)),
+                dma((3,)),
+                dma((n_items,)),
+                dma((2, (n_blocks + 1) // 2)),
+                pltpu.VMEM((3, depth // 2, wide), jnp.float32),
+                dma((2, 3)),
             ],
             compiler_params=pltpu.CompilerParams(
                 collective_id=0, has_side_effects=True, vmem_limit_bytes=44 * 1024 * 1024

time: 72.5 us -> 71.1 us (0.981)
  Pallas kernels: 71.7 us -> 70.3 us
    pallas_call x1, Pallas kernels: 65.7 us -> 64.2 us  [shards(): pl.pallas_call(lambda *refs: kernel(n_rows, n_width, pieces_of, cross_fir...]
where the time goes in v6:
time: 71.1 us; the launch traced here: 70.9 us
  Pallas kernels  70.3 us (99%)
    pallas_call x1, Pallas kernels, shards(): pl.pallas_call(lambda *refs: kernel(n_rows, n_width, pieces_of, cross_fir...  64.2 us
    pallas_call x1, Pallas kernels, shards(): pl.pallas_call(lambda *refs: store(pieces_of, wide, *refs), out_shape=(ja...  6.04 us

profile of v6, /device:TPU:1, one launch (start us, length us, event | category | flops | bytes accessed | tf_op | source)
XLA Modules:
  0.0 70.9 jit_solution(15233968009487586211)
XLA Ops:
  0.6 64.2 %shard_map.144 = (bf16[7168,256]{1,0:T(8,128)(2,1)S(1)}, bf16[7168,256]{1,0:T(8,128)(2,1)S(1)}, bf16[7168,128]{1,0:T(8,128)(2,1)S(1)}, bf16[7168,256]{1,0:T(8,12...) custom-call(f32[448]{0:T(512)} %refs_0_.1, ...), custom_call_target="tpu_custom_call" | custom-call | tf_op jit(solution)/shard_map/pallas_call | solution.py:524
  64.9 6.0 %shard_map.145 = (bf16[7168,896]{1,0:T(8,128)(2,1)}, bf16[7168,128]{1,0:T(8,128)(2,1)}, bf16[7168,128]{1,0:T(8,128)(2,1)}, f32[896]{0:T(1024)}, f32[128]{0:T(128)}, /*index=5*/f32[128]{0:T(128)}, bf16[7168]{0:T(1024)(128)(2,1)}) custom-call(bf16[7168,256]{1,0:T(8,128)(2,1)S(1)} %get-tuple-element.16.refs_0_, ...), custom_call_target="tpu_custom_call" | custom-call | tf_op jit(solution)/shard_map/pallas_call | solution.py:556

commit v7 on v6

--- a/solution.py
+++ b/solution.py
@@ -25,12 +25,12 @@
     return blocks, [b for b, pieces in enumerate(blocks) if pieces[0] < first]
 
 
-def ahead_of(blocks, cross_first):
+def ahead_of(cross_first):
     last = cross_first[-1]
-    return {(UP, 0, 1, last): 0, (DOWN, 0, 1, last): 1, (ACROSS, 0, 0, last): 0}
-
-
-def plan(weights, cross_first, ahead):
+    return (UP, 0, 1, last), (DOWN, 0, 1, last), (ACROSS, 0, 0, last)
+
+
+def plan(weights, cross_first, ahead, gone):
     free, flying, ready = [0.0] * 3, [0] * 3, [[], [], []]
     events, order, clock = [], [], [0]
 
@@ -63,8 +63,8 @@
             while ready[link] and flying[link] < DEPTH:
                 item = ready[link].pop(0)[2]
                 flying[link] += 1
-                size = weights[item[3]] * (1.0 if is_whole(item) and item not in ahead else 0.5)
-                free[link] = max(free[link], now) + size
+                size = 1.0 - gone if item in ahead else 1.0 if is_whole(item) else 0.5
+                free[link] = max(free[link], now) + size * weights[item[3]]
                 put(free[link] + LAG, item)
                 sends.append(item)
         order.append((event, sends))
@@ -127,7 +127,7 @@
     count = len(groups)
     tile = 64 if depth % 64 == 0 else 16
     half = depth // 2
-    step_rows = 32 if half % 32 == 0 else 16
+    step_rows = 32
 
     def drain(ref, sem):
         pltpu.make_async_copy(ref, ref, sem).wait()
@@ -137,8 +137,7 @@
         small.append(pltpu.make_async_copy(src, dst, small_sem.at[i]))
         small[-1].start()
 
-    kinds = [cross_first, [b for b in range(len(blocks)) if b not in cross_first]]
-    early = [p for kind in kinds for p in pieces_of[kind[0]]]
+    early = pieces_of[len(cross_first)]
     (first_out,) = pieces_of[cross_first[-1]]
     late = [first_out] + [p for p in range(count) if p not in early + [first_out]]
     loading = early + late
@@ -226,9 +225,10 @@
     twin = me + 1 - 2 * core
     target = {UP: device(0, 1), DOWN: device(0, -1), ACROSS: device(1, 0)}
     sum_up(first_out)
-    for item, way in ahead.items():
+    gone = stage.shape[1]
+    for item in ahead:
         pltpu.make_async_remote_copy(
-            src_ref=mixed.at[first_out, 0, pl.ds(way * half, half), :],
+            src_ref=mixed.at[first_out, 0, pl.ds(0, gone), :],
             dst_ref=stage.at[item[0]],
             send_sem=stage_sem.at[0, item[0]],
             recv_sem=stage_sem.at[1, item[0]],
@@ -245,7 +245,7 @@
             slots[event] = len(slots)
 
     def size_of(item):
-        return depth if is_whole(item) and item not in ahead else half
+        return depth - gone if item in ahead else depth if is_whole(item) else half
 
     def whole(owner):
         return pl.ds(pl.multiple_of(owner * depth, half), depth)
@@ -265,7 +265,7 @@
     def rows_of(item, sender):
         owner, way = held(item, sender)
         if item in ahead:
-            way = 1 - ahead[item]
+            return pl.ds(pl.multiple_of(owner * depth + gone, 32), depth - gone)
         return whole(owner) if way is None else part_of(owner, way)
 
     def remote(item, sender):
@@ -311,7 +311,7 @@
     def take_in(item):
         link, _, _, g = item
         drain(stage.at[link], stage_sem.at[1, link])
-        start = held(item, False)[0] * depth + ahead[item] * half
+        start = held(item, False)[0] * depth
         by = late_scales[1][:1, :]
 
         def narrow(i, carry):
@@ -320,7 +320,7 @@
             blocks[g][here, :] = (stage[link, rows, :] * by).astype(blocks[g].dtype)
             return carry
 
-        lax.fori_loop(0, half // step_rows, narrow, 0)
+        lax.fori_loop(0, gone // step_rows, narrow, 0)
 
     def make_block(g):
         pieces, out = pieces_of[g], blocks[g]
@@ -504,10 +504,11 @@
         count = 2 + wide_query // wide
         pieces_of, cross_first = layout(count)
         n_blocks = len(pieces_of)
-        ahead = ahead_of(pieces_of, cross_first)
-        schedule = plan([len(pieces) for pieces in pieces_of], cross_first, ahead)
+        ahead = ahead_of(cross_first)
+        gone = depth * 5 // 7 // 32 * 32
+        schedule = plan([len(pieces) for pieces in pieces_of], cross_first, ahead, gone / depth)
         n_items = len(schedule) - n_blocks
-        n_early = len(pieces_of[0]) + len(pieces_of[len(cross_first)])
+        n_early = len(pieces_of[len(cross_first)])
         piece = norm_train.shape[0]
         total = depth * n_rows
         hbm = pl.BlockSpec(memory_space=pltpu.HBM)
@@ -546,7 +547,7 @@
                 dma((3,)),
                 dma((n_items,)),
                 dma((2, (n_blocks + 1) // 2)),
-                pltpu.VMEM((3, depth // 2, wide), jnp.float32),
+                pltpu.VMEM((3, gone, wide), jnp.float32),
                 dma((2, 3)),
             ],
             compiler_params=pltpu.CompilerParams(

time: 71.1 us -> 71 us (level)
  no operation moved by 1% of the time
where the time goes in v7:
time: 71 us; the launch traced here: 70.9 us
  Pallas kernels  70.2 us (99%)
    pallas_call x1, Pallas kernels, shards(): pl.pallas_call(lambda *refs: kernel(n_rows, n_width, pieces_of, cross_fir...  64.2 us
    pallas_call x1, Pallas kernels, shards(): pl.pallas_call(lambda *refs: store(pieces_of, wide, *refs), out_shape=(ja...  6.04 us

profile of v7, /device:TPU:1, one launch (start us, length us, event | category | flops | bytes accessed | tf_op | source)
XLA Modules:
  0.0 70.9 jit_solution(6943374351588424686)
XLA Ops:
  0.6 64.2 %shard_map.144 = (bf16[7168,256]{1,0:T(8,128)(2,1)S(1)}, bf16[7168,256]{1,0:T(8,128)(2,1)S(1)}, bf16[7168,128]{1,0:T(8,128)(2,1)S(1)}, bf16[7168,256]{1,0:T(8,12...) custom-call(f32[448]{0:T(512)} %refs_0_.1, ...), custom_call_target="tpu_custom_call" | custom-call | tf_op jit(solution)/shard_map/pallas_call | solution.py:525
  64.8 6.0 %shard_map.145 = (bf16[7168,896]{1,0:T(8,128)(2,1)}, bf16[7168,128]{1,0:T(8,128)(2,1)}, bf16[7168,128]{1,0:T(8,128)(2,1)}, f32[896]{0:T(1024)}, f32[128]{0:T(128)}, /*index=5*/f32[128]{0:T(128)}, bf16[7168]{0:T(1024)(128)(2,1)}) custom-call(bf16[7168,256]{1,0:T(8,128)(2,1)S(1)} %get-tuple-element.16.refs_0_, ...), custom_call_target="tpu_custom_call" | custom-call | tf_op jit(solution)/shard_map/pallas_call | solution.py:557

commit v8 on v7

--- a/solution.py
+++ b/solution.py
@@ -45,7 +45,7 @@
     first = cross_first
     second = [b for b in range(len(weights)) if b not in cross_first]
     for k in range(max(len(first), len(second))):
-        for b in second[k : k + 1] + first[k : k + 1]:
+        for b in first[k : k + 1] + second[k : k + 1]:
             put(0.1 * len(events), b)
     while events:
         events.sort()
@@ -69,6 +69,12 @@
                 sends.append(item)
         order.append((event, sends))
     return order
+
+
+def arrival(item, cross_first):
+    link, far, hop, block = item
+    together = link != ACROSS and hop == 2 and block in cross_first
+    return (UP, far, hop, block) if together else item
 
 
 def steps_after(item, cross_first):
@@ -137,7 +143,7 @@
         small.append(pltpu.make_async_copy(src, dst, small_sem.at[i]))
         small[-1].start()
 
-    early = pieces_of[len(cross_first)]
+    early = pieces_of[0]
     (first_out,) = pieces_of[cross_first[-1]]
     late = [first_out] + [p for p in range(count) if p not in early + [first_out]]
     loading = early + late
@@ -242,7 +248,7 @@
     slots = {}
     for event, _ in schedule:
         if not isinstance(event, int):
-            slots[event] = len(slots)
+            slots.setdefault(arrival(event, cross_first), len(slots))
 
     def size_of(item):
         return depth - gone if item in ahead else depth if is_whole(item) else half
@@ -275,7 +281,7 @@
             src_ref=ref,
             dst_ref=ref,
             send_sem=send_sem.at[link],
-            recv_sem=recv_sem.at[slots[item]],
+            recv_sem=recv_sem.at[slots[arrival(item, cross_first)]],
             device_id={"rows": target[link]},
             device_id_type=MESH,
         )
@@ -420,6 +426,7 @@
                 relay(way).start()
 
     moments = [len(schedule) * (3 + i) // 12 for i in range(len(duties))]
+    halves = set()
     meeting, swapping = len(blocks), (len(blocks) + moments[0]) // 2
     for index, (event, items) in enumerate(schedule):
         if index == meeting:
@@ -436,12 +443,22 @@
         else:
             if event in ahead:
                 take_in(event)
-            remote(event, False).wait_recv()
-            g = event[3]
-            rows = whole(held(event, False)[0]) if event in ahead else rows_of(event, False)
+            g, rows = event[3], rows_of(event, False)
+            known = arrival(event, cross_first)
+            if is_whole(event) or g not in cross_first:
+                remote(event, False).wait_recv()
+            elif known in halves:
+                rows = whole(held(event, False)[0])
+                drain(blocks[g].at[rows, :], recv_sem.at[slots[known]])
+            else:
+                halves.add(known)
+                rows = None
+            if event in ahead:
+                rows = whole(held(event, False)[0])
         for item in items:
             send(item)
-        share_with_twin(g, rows)
+        if rows is not None:
+            share_with_twin(g, rows)
 
     def drain_rows(rows, sem):
         drain(blocks[0].at[pl.ds(0, rows // len(pieces_of[0])), :], sem)
@@ -507,8 +524,8 @@
         ahead = ahead_of(cross_first)
         gone = depth * 5 // 7 // 32 * 32
         schedule = plan([len(pieces) for pieces in pieces_of], cross_first, ahead, gone / depth)
-        n_items = len(schedule) - n_blocks
-        n_early = len(pieces_of[len(cross_first)])
+        n_items = len({arrival(e, cross_first) for e, _ in schedule if not isinstance(e, int)})
+        n_early = len(pieces_of[0])
         piece = norm_train.shape[0]
         total = depth * n_rows
         hbm = pl.BlockSpec(memory_space=pltpu.HBM)
@@ -564,7 +581,7 @@
             + tuple(jax.ShapeDtypeStruct(o.shape, o.dtype) for o in out_shape[n_blocks:]),
             in_specs=[vmem] * (n_blocks + 4),
             out_specs=[hbm] * 7,
-            scratch_shapes=[dma((count + 4,))],
+            scratch_shapes=[dma((n_blocks + 5,))],
             compiler_params=pltpu.CompilerParams(vmem_limit_bytes=1024 * 1024),
         )(*gathered)
 

time: 71 us -> 70.9 us (level)
  no operation moved by 1% of the time
where the time goes in v8:
time: 70.9 us; the launch traced here: 70.8 us
  Pallas kernels  70.1 us (99%)
    pallas_call x1, Pallas kernels, shards(): pl.pallas_call(lambda *refs: kernel(n_rows, n_width, pieces_of, cross_fir...  64.1 us
    pallas_call x1, Pallas kernels, shards(): pl.pallas_call(lambda *refs: store(pieces_of, wide, *refs), out_shape=(ja...  6.01 us

profile of v8, /device:TPU:1, one launch (start us, length us, event | category | flops | bytes accessed | tf_op | source)
XLA Modules:
  0.0 70.8 jit_solution(12226767692743621226)
XLA Ops:
  0.6 64.1 %shard_map.144 = (bf16[7168,256]{1,0:T(8,128)(2,1)S(1)}, bf16[7168,256]{1,0:T(8,128)(2,1)S(1)}, bf16[7168,128]{1,0:T(8,128)(2,1)S(1)}, bf16[7168,256]{1,0:T(8,12...) custom-call(f32[448]{0:T(512)} %refs_0_.1, ...), custom_call_target="tpu_custom_call" | custom-call | tf_op jit(solution)/shard_map/pallas_call | solution.py:542
  64.8 6.0 %shard_map.145 = (bf16[7168,896]{1,0:T(8,128)(2,1)}, bf16[7168,128]{1,0:T(8,128)(2,1)}, bf16[7168,128]{1,0:T(8,128)(2,1)}, f32[896]{0:T(1024)}, f32[128]{0:T(128)}, /*index=5*/f32[128]{0:T(128)}, bf16[7168]{0:T(1024)(128)(2,1)}) custom-call(bf16[7168,256]{1,0:T(8,128)(2,1)S(1)} %get-tuple-element.16.refs_0_, ...), custom_call_target="tpu_custom_call" | custom-call | tf_op jit(solution)/shard_map/pallas_call | solution.py:574

commit v9 on v7

--- a/solution.py
+++ b/solution.py
@@ -441,7 +441,11 @@
             rows = whole(held(event, False)[0]) if event in ahead else rows_of(event, False)
         for item in items:
             send(item)
-        share_with_twin(g, rows)
+        if not isinstance(event, int):
+            share_with_twin(g, rows)
+        if index == 2 * len(blocks):
+            for b in range(len(blocks)):
+                share_with_twin(b, whole(me))
 
     def drain_rows(rows, sem):
         drain(blocks[0].at[pl.ds(0, rows // len(pieces_of[0])), :], sem)

time: 71 us -> 71 us (level)
  no operation moved by 1% of the time
where the time goes in v9:
time: 71 us; the launch traced here: 70.9 us
  Pallas kernels  70.2 us (99%)
    pallas_call x1, Pallas kernels, shards(): pl.pallas_call(lambda *refs: kernel(n_rows, n_width, pieces_of, cross_fir...  64.2 us
    pallas_call x1, Pallas kernels, shards(): pl.pallas_call(lambda *refs: store(pieces_of, wide, *refs), out_shape=(ja...  6.04 us

profile of v9, /device:TPU:1, one launch (start us, length us, event | category | flops | bytes accessed | tf_op | source)
XLA Modules:
  0.0 70.9 jit_solution(4516351063894866460)
XLA Ops:
  0.6 64.2 %shard_map.144 = (bf16[7168,256]{1,0:T(8,128)(2,1)S(1)}, bf16[7168,256]{1,0:T(8,128)(2,1)S(1)}, bf16[7168,128]{1,0:T(8,128)(2,1)S(1)}, bf16[7168,256]{1,0:T(8,12...) custom-call(f32[448]{0:T(512)} %refs_0_.1, ...), custom_call_target="tpu_custom_call" | custom-call | tf_op jit(solution)/shard_map/pallas_call | solution.py:529
  64.8 6.0 %shard_map.145 = (bf16[7168,896]{1,0:T(8,128)(2,1)}, bf16[7168,128]{1,0:T(8,128)(2,1)}, bf16[7168,128]{1,0:T(8,128)(2,1)}, f32[896]{0:T(1024)}, f32[128]{0:T(128)}, /*index=5*/f32[128]{0:T(128)}, bf16[7168]{0:T(1024)(128)(2,1)}) custom-call(bf16[7168,256]{1,0:T(8,128)(2,1)S(1)} %get-tuple-element.16.refs_0_, ...), custom_call_target="tpu_custom_call" | custom-call | tf_op jit(solution)/shard_map/pallas_call | solution.py:561

commit v10 on v7

--- a/solution.py
+++ b/solution.py
@@ -44,9 +44,8 @@
 
     first = cross_first
     second = [b for b in range(len(weights)) if b not in cross_first]
-    for k in range(max(len(first), len(second))):
-        for b in second[k : k + 1] + first[k : k + 1]:
-            put(0.1 * len(events), b)
+    for b in (3, 0, 1, 4, 2):
+        put(0.1 * len(events), b)
     while events:
         events.sort()
         now, _, event = events.pop(0)
@@ -137,7 +136,7 @@
         small.append(pltpu.make_async_copy(src, dst, small_sem.at[i]))
         small[-1].start()
 
-    early = pieces_of[len(cross_first)]
+    early = pieces_of[3]
     (first_out,) = pieces_of[cross_first[-1]]
     late = [first_out] + [p for p in range(count) if p not in early + [first_out]]
     loading = early + late
@@ -508,7 +507,7 @@
         gone = depth * 5 // 7 // 32 * 32
         schedule = plan([len(pieces) for pieces in pieces_of], cross_first, ahead, gone / depth)
         n_items = len(schedule) - n_blocks
-        n_early = len(pieces_of[len(cross_first)])
+        n_early = len(pieces_of[3])
         piece = norm_train.shape[0]
         total = depth * n_rows
         hbm = pl.BlockSpec(memory_space=pltpu.HBM)
@@ -564,7 +563,7 @@
             + tuple(jax.ShapeDtypeStruct(o.shape, o.dtype) for o in out_shape[n_blocks:]),
             in_specs=[vmem] * (n_blocks + 4),
             out_specs=[hbm] * 7,
-            scratch_shapes=[dma((count + 4,))],
+            scratch_shapes=[dma((n_blocks + 5,))],
             compiler_params=pltpu.CompilerParams(vmem_limit_bytes=1024 * 1024),
         )(*gathered)
 

time: 71 us -> 71 us (level)
  no operation moved by 1% of the time
where the time goes in v10:
time: 71 us; the launch traced here: 70.8 us
  Pallas kernels  70.2 us (99%)
    pallas_call x1, Pallas kernels, shards(): pl.pallas_call(lambda *refs: kernel(n_rows, n_width, pieces_of, cross_fir...  64.2 us
    pallas_call x1, Pallas kernels, shards(): pl.pallas_call(lambda *refs: store(pieces_of, wide, *refs), out_shape=(ja...  6.01 us

profile of v10, /device:TPU:1, one launch (start us, length us, event | category | flops | bytes accessed | tf_op | source)
XLA Modules:
  0.0 70.8 jit_solution(4863225875697759982)
XLA Ops:
  0.6 64.2 %shard_map.144 = (bf16[7168,256]{1,0:T(8,128)(2,1)S(1)}, bf16[7168,256]{1,0:T(8,128)(2,1)S(1)}, bf16[7168,128]{1,0:T(8,128)(2,1)S(1)}, bf16[7168,256]{1,0:T(8,12...) custom-call(f32[448]{0:T(512)} %refs_0_.1, ...), custom_call_target="tpu_custom_call" | custom-call | tf_op jit(solution)/shard_map/pallas_call | solution.py:524
  64.8 6.0 %shard_map.145 = (bf16[7168,896]{1,0:T(8,128)(2,1)}, bf16[7168,128]{1,0:T(8,128)(2,1)}, bf16[7168,128]{1,0:T(8,128)(2,1)}, f32[896]{0:T(1024)}, f32[128]{0:T(128)}, /*index=5*/f32[128]{0:T(128)}, bf16[7168]{0:T(1024)(128)(2,1)}) custom-call(bf16[7168,256]{1,0:T(8,128)(2,1)S(1)} %get-tuple-element.16.refs_0_, ...), custom_call_target="tpu_custom_call" | custom-call | tf_op jit(solution)/shard_map/pallas_call | solution.py:556
